TPU v7x, 32 devices: a whole 2x2x4 slice. The times are simulated.
32 devices in a mesh: leaf: 16 (over z, y, x), blk: 2 (over core).
Axes of the slice: x: 2, y: 2, z: 4, core: 2. Of those that a mesh axis runs over, the one named last changes fastest.
Arguments:
- sketch: bfloat16 [16384, 512], P(('leaf', 'blk')), may hold values from -6 to 6
- near_block: bfloat16 [16384, 1024], P(('leaf', 'blk')), may hold values from -0.125 to 0.125
- next_block: bfloat16 [16384, 1024], P(('leaf', 'blk')), may hold values from -0.125 to 0.125
- link_own: bfloat16 [4096, 1024], P('leaf', 'blk')
- link_next: bfloat16 [4096, 1024], P('leaf', 'blk')
- diag_block: float32 [4096, 128], P(('leaf', 'blk'))
- sub_block: float32 [4096, 128], P(('leaf', 'blk'))
- leaf_skeleton: int32 [16, 128], P('leaf'), may hold values from 0 to 1023, as said below
- merge_skeleton: int32 [16, 4, 128], P('leaf'), may hold values from 0 to 255, as said below
Outputs:
- samples: float32 [16384, 512], P(('leaf', 'blk'))
- leaf_interp: float32 [16384, 128], P(('leaf', 'blk'))
- merge_interp: float32 [32, 4, 256, 128], P(('leaf', 'blk'))
Inputs may be any that keep to these rules, and one draw needn't show every extreme that they name: `leaf_skeleton`: each row holds 128 distinct numbers. `merge_skeleton`: for each row p and level index j, the 128 numbers are distinct; rows p and q with p // 2^(j+1) == q // 2^(j+1) hold equal entries at level index j.
All inputs are finite; a program needn't handle non-finite values.
Results may differ from a plain program's by a relative error of at most 0.0027.
Values may be sent and summed in bfloat16 or wider, within the bound.
A program may use at most 64 MiB of HBM per device.

v0:
```python
import jax
import jax.numpy as jnp
from jax import lax
from jax.sharding import PartitionSpec as P

highest = lax.Precision.HIGHEST


def shifted(block, axis, distance):
    devices = range(lax.axis_size(axis))
    route = [((i - distance) % len(devices), i) for i in devices]
    return lax.ppermute(block, axis, route)


def carried_in(value, axis, join, neutral, backward):
    count, mine = (lax.axis_size(axis), lax.axis_index(axis))
    pieces = jax.tree.map(lambda part: lax.all_gather(part, axis), value)
    if backward:
        pieces = jax.tree.map(lambda part: part[::-1], pieces)
        mine = count - 1 - mine
    total = jax.tree.map(
        lambda part, zero: jnp.full_like(part, 0) + jnp.asarray(zero, part.dtype), value, neutral
    )

    def step(position, total):
        longer = join(total, jax.tree.map(lambda part: part[position], pieces))
        return jax.tree.map(lambda new, old: jnp.where(position < mine, new, old), longer, total)

    return lax.fori_loop(0, count - 1, step, total)


def from_partner(block, axis, apart):
    count = lax.axis_size(axis)
    route = []
    for low in range(count):
        high = low | 1 << apart
        if high != low and high < count:
            route += [(low, high), (high, low)]
    return lax.ppermute(block, axis, route)


def interp_rows(candidates, chosen):
    gram_matrix = jnp.dot(chosen, chosen.T, precision=highest)
    factor = jnp.linalg.cholesky(gram_matrix)
    cross_term = jnp.dot(chosen, candidates.T, precision=highest)
    return jax.scipy.linalg.cho_solve((factor, True), cross_term).T


def compose(earlier, latter):
    return (
        jnp.dot(latter[0], earlier[0], precision=highest),
        jnp.dot(latter[0], earlier[1], precision=highest) + latter[1],
    )


def per_device(
    sketch,
    near_block,
    next_block,
    link_own,
    link_next,
    diag_block,
    sub_block,
    leaf_skeleton,
    merge_skeleton,
):
    row_count = sketch.shape[0]
    blk_count = lax.axis_size("blk")
    blk_position = lax.axis_index("blk")
    whole_group = lax.all_gather(sketch, "blk", axis=0, tiled=True)
    following_group = shifted(whole_group, "leaf", -1)
    direct = jnp.dot(near_block, whole_group, preferred_element_type=jnp.float32) + jnp.dot(
        next_block, following_group, preferred_element_type=jnp.float32
    )
    following_rows = lax.dynamic_slice_in_dim(
        following_group, blk_position * row_count, row_count, 0
    )
    own_part = link_own
    next_part = link_next
    rhs_load = lax.psum_scatter(
        jnp.dot(own_part, sketch, preferred_element_type=jnp.float32)
        + jnp.dot(next_part, following_rows, preferred_element_type=jnp.float32),
        "blk",
        scatter_dimension=0,
        tiled=True,
    )
    step_map = -jax.scipy.linalg.solve_triangular(diag_block, sub_block, lower=True)
    start_value = jax.scipy.linalg.solve_triangular(diag_block, rhs_load, lower=True)
    identity = (jnp.eye(step_map.shape[0], dtype=jnp.float32), jnp.zeros_like(rhs_load))
    prefix = carried_in((step_map, start_value), "blk", compose, identity, False)
    solved = start_value + jnp.dot(step_map, prefix[1], precision=highest)
    back_map = step_map.T
    back_prefix = carried_in(
        (back_map, -jnp.dot(back_map, solved, precision=highest)), "blk", compose, identity, True
    )
    back_solved = jax.scipy.linalg.solve_triangular(
        diag_block, solved - back_prefix[1], lower=True, trans="T"
    )
    weights = back_solved.astype(jnp.bfloat16)
    contract_rows = (((0,), (0,)), ((), ()))
    block_rows = lax.all_gather(weights, "blk", axis=0, tiled=True)
    own_part = link_own
    next_part = link_next
    own_back = lax.dot_general(
        own_part, block_rows, contract_rows, preferred_element_type=jnp.float32
    )
    next_back = lax.dot_general(
        next_part, block_rows, contract_rows, preferred_element_type=jnp.float32
    )
    from_previous = shifted(next_back, "leaf", 1)
    samples = direct - own_back - from_previous
    upper_half = blk_position % 2
    pair_row = blk_position // 2
    leaf_set = lax.dynamic_index_in_dim(leaf_skeleton, pair_row, 0, keepdims=False)
    partner = from_partner(samples, "blk", 0)
    leaf_rows = jnp.where(
        upper_half == 0,
        jnp.concatenate([samples, partner], axis=0),
        jnp.concatenate([partner, samples], axis=0),
    )
    chosen = jnp.take(leaf_rows, leaf_set, axis=0)
    leaf_interp = interp_rows(samples, chosen)
    flat_index = lax.axis_index("leaf") * blk_count + blk_position
    own_sets = lax.dynamic_index_in_dim(merge_skeleton, pair_row, 0, keepdims=False)
    results = []
    for level_index in range(own_sets.shape[0]):
        sibling = from_partner(chosen, ("leaf", "blk"), level_index + 1)
        is_upper = flat_index // (2 << level_index) % 2
        candidates = jnp.where(
            is_upper == 0,
            jnp.concatenate([chosen, sibling], axis=0),
            jnp.concatenate([sibling, chosen], axis=0),
        )
        chosen = jnp.take(candidates, own_sets[level_index], axis=0)
        results.append(interp_rows(candidates, chosen))
    merge_interp = jnp.stack(results, axis=0)[None]
    return (samples, leaf_interp, merge_interp)


def solution(mesh):
    placed = (
        P(("leaf", "blk"), None),
        P(("leaf", "blk"), None),
        P(("leaf", "blk"), None),
        P("leaf", "blk"),
        P("leaf", "blk"),
        P(("leaf", "blk"), None),
        P(("leaf", "blk"), None),
        P("leaf", None),
        P("leaf", None, None),
    )
    return jax.shard_map(
        per_device,
        mesh=mesh,
        in_specs=placed,
        out_specs=(
            P(("leaf", "blk"), None),
            P(("leaf", "blk"), None),
            P(("leaf", "blk"), None, None, None),
        ),
        check_vma=False,
    )
```

profile of v0, /device:TPU:0, one launch (start us, length us, event | category | flops | bytes accessed | tf_op | source)
XLA Modules:
  0.0 254.1 jit_solution(4499632299349130157)
XLA Ops:
  8.0 13.4 %all-gather.6.cloned.1.call-done = bf16[1024,512]{1,0:T(8,128)(2,1)} async-done(((bf16[512,512]{1,0:T(8,128)(2,1)}), bf16[1024,512]{1,0:T(8,128)(2,1)}) %all-gather.6.cloned.1.call-update) | async-done | bytes 1048592 | tf_op jit(solution)/shard_map/all_gather | solution.py:70
  21.3 5.4 %collective-permute-start = (bf16[1024,512]{1,0:T(8,128)(2,1)}, bf16[1024,512]{1,0:T(8,128)(2,1)S(1)}, u32[]{:S(2)}, u32[]{:S(2)}) collective-permute-start(bf16[1024,512]{1,0:T(8,128)(2,1)} %all-gather.6.cloned.1.call-done), channel_id=1, source_target_pairs={{2,0},{4,2},{6,4},{8,6},{10,8},{12,10},{14,12},{16,14},{18,16},{20... | collective-permute-start | bytes 3145736 | tf_op jit(solution)/shard_map/ppermute | solution.py:12
  28.2 21.8 %collective-permute-done = bf16[1024,512]{1,0:T(8,128)(2,1)S(1)} collective-permute-done((bf16[1024,512]{1,0:T(8,128)(2,1)}, bf16[1024,512]{1,0:T(8,128)(2,1)S(1)}, u32[]{:S(2)}, u32[]{:S(2)}) %collective-permute-start) | collective-permute-done | bytes 1048608 | tf_op jit(solution)/shard_map/ppermute | solution.py:12
  49.9 2.0 fusion.2
  52.0 9.8 %custom-call.24 = f32[1,128,128]{1,2,0:T(8,128)S(1)} custom-call(f32[1,128,128]{2,1,0:T(8,128)S(1)} %select_bitcast_fusion), custom_call_target="InvertDiagBlocksLowerTriangular" | custom-call | tf_op jit(solution)/shard_map/jit(_solve_triangular)/triangular_solve/custom-call.3 | solution.py:96
  62.2 1.9 all-gather
  64.1 1.9 all-gather.2
  67.3 2.2 all-gather.1
  70.6 2.3 all-gather.3
  73.6 2.0 all_gather.39
  77.3 28.3 %collective-permute-done.1 = f32[512,512]{1,0:T(8,128)S(1)} collective-permute-done((f32[512,512]{1,0:T(8,128)S(1)}, f32[512,512]{1,0:T(8,128)S(1)}, u32[]{:S(2)}, u32[]{:S(2)}) %collective-permute-start.1) | collective-permute-done | bytes 1048608 | tf_op jit(solution)/shard_map/ppermute | solution.py:12
  106.7 2.4 collective-permute-done.2
  110.7 2.5 gather_fusion
  115.1 11.7 %cholesky.89 = f32[128,128]{1,0:T(8,128)S(1)} custom-call(f32[128,128]{1,0:T(8,128)S(1)} %fusion.43), custom_call_target="Cholesky" | custom-call | tf_op jit(solution)/shard_map/jit(cholesky)/cholesky | solution.py:44
  128.1 9.8 %custom-call.26 = f32[1,128,128]{1,2,0:T(8,128)S(1)} custom-call(f32[1,128,128]{2,1,0:T(8,128)S(1)} %fusion.17), custom_call_target="InvertDiagBlocksLowerTriangular" | custom-call | tf_op jit(solution)/shard_map/jit(_cho_solve)/triangular_solve/custom-call.3 | solution.py:46
  141.7 11.9 %cholesky.100 = f32[128,128]{1,0:T(8,128)S(1)} custom-call(f32[128,128]{1,0:T(8,128)S(1)} %fusion.39), custom_call_target="Cholesky" | custom-call | tf_op jit(solution)/shard_map/jit(cholesky)/cholesky | solution.py:44
  155.0 9.8 %custom-call.27 = f32[1,128,128]{1,2,0:T(8,128)S(1)} custom-call(f32[1,128,128]{2,1,0:T(8,128)S(1)} %fusion.18), custom_call_target="InvertDiagBlocksLowerTriangular" | custom-call | tf_op jit(solution)/shard_map/jit(_cho_solve)/triangular_solve | solution.py:46
  167.6 11.7 %cholesky.111 = f32[128,128]{1,0:T(8,128)S(1)} custom-call(f32[128,128]{1,0:T(8,128)S(1)} %fusion.35), custom_call_target="Cholesky" | custom-call | tf_op jit(solution)/shard_map/jit(cholesky)/cholesky | solution.py:44
  180.6 10.2 %custom-call.28 = f32[1,128,128]{1,2,0:T(8,128)S(1)} custom-call(f32[1,128,128]{2,1,0:T(8,128)S(1)} %fusion.19), custom_call_target="InvertDiagBlocksLowerTriangular" | custom-call | tf_op jit(solution)/shard_map/jit(_cho_solve)/triangular_solve | solution.py:46
  193.4 3.4 %collective-permute-start.6 = (f32[128,512]{1,0:T(8,128)S(1)}, f32[128,512]{1,0:T(8,128)S(1)}, u32[]{:S(2)}, u32[]{:S(2)}) collective-permute-start(f32[128,512]{1,0:T(8,128)S(1)} %broadcast_select_fusion), channel_id=1, source_target_pairs={{0,16},{16,0},{1,17},{17,1},{2,18},{18,2},{3,19},{19,3},{4,20},{20... | collective-permute-start | bytes 786440 | tf_op jit(solution)/shard_map/ppermute | solution.py:39
  196.9 11.7 %cholesky.122 = f32[128,128]{1,0:T(8,128)S(1)} custom-call(f32[128,128]{1,0:T(8,128)S(1)} %fusion.31), custom_call_target="Cholesky" | custom-call | tf_op jit(solution)/shard_map/jit(cholesky)/cholesky | solution.py:44
  210.0 9.8 %custom-call.29 = f32[1,128,128]{1,2,0:T(8,128)S(1)} custom-call(f32[1,128,128]{2,1,0:T(8,128)S(1)} %fusion.20), custom_call_target="InvertDiagBlocksLowerTriangular" | custom-call | tf_op jit(solution)/shard_map/jit(_cho_solve)/triangular_solve | solution.py:46
  222.5 11.9 %cholesky.133 = f32[128,128]{1,0:T(8,128)S(1)} custom-call(f32[128,128]{1,0:T(8,128)S(1)} %fusion.27), custom_call_target="Cholesky" | custom-call | tf_op jit(solution)/shard_map/jit(cholesky)/cholesky | solution.py:44
  235.7 9.8 %custom-call.30 = f32[1,128,128]{1,2,0:T(8,128)S(1)} custom-call(f32[1,128,128]{2,1,0:T(8,128)S(1)} %fusion.21), custom_call_target="InvertDiagBlocksLowerTriangular" | custom-call | tf_op jit(solution)/shard_map/jit(_cho_solve)/triangular_solve | solution.py:46
  (116 shorter events, 31.4 us)
Async XLA Ops:
  7.2 69.1 %copy-start = (bf16[512,1024]{1,0:T(8,128)(2,1)S(1)}, bf16[512,1024]{1,0:T(8,128)(2,1)}, u32[]{:S(2)}) copy-start(bf16[512,1024]{1,0:T(8,128)(2,1)} %param.19) | copy-start | bytes 3145732
  7.2 44.8 %copy-start.6 = (f32[128,128]{1,0:T(8,128)S(1)}, f32[128,128]{1,0:T(8,128)}, u32[]{:S(2)}) copy-start(f32[128,128]{1,0:T(8,128)} %param.23) | copy-start | bytes 196612
  7.2 54.7 %copy-start.5 = (f32[128,128]{1,0:T(8,128)S(1)}, f32[128,128]{1,0:T(8,128)}, u32[]{:S(2)}) copy-start(f32[128,128]{1,0:T(8,128)} %param.24) | copy-start | bytes 196612
  7.2 14.1 %all-gather.6.cloned.1.call-start = ((), (), s32[]{:S(2)}) async-start(), calls=%async_computation.1 | async-start | bytes 1572864 | tf_op jit(solution)/shard_map/all_gather | solution.py:70
  7.9 58.0 %reduce-scatter.2.cloned.1.call-start = ((), (), s32[]{:S(2)}) async-start(), calls=%async_computation.2 | async-start | bytes 786432 | tf_op jit(solution)/shard_map/reduce_scatter | solution.py:80
  21.3 28.6 %collective-permute-start = (bf16[1024,512]{1,0:T(8,128)(2,1)}, bf16[1024,512]{1,0:T(8,128)(2,1)S(1)}, u32[]{:S(2)}, u32[]{:S(2)}) collective-permute-start(bf16[1024,512]{1,0:T(8,128)(2,1)} %all-gather.6.cloned.1.call-done), channel_id=1, source_target_pairs={{2,0},{4,2},{6,4},{8,6},{10,8},{12,10},{14,12},{16,14},{18,16},{20... | collective-permute-start | bytes 3145736 | tf_op jit(solution)/shard_map/ppermute | solution.py:12
  69.8 5.8 %copy-start.4 = (bf16[256,512]{1,0:T(8,128)(2,1)S(1)}, bf16[256,512]{1,0:T(8,128)(2,1)}, u32[]{:S(2)}) copy-start(bf16[256,512]{1,0:T(8,128)(2,1)} %param.22) | copy-start | bytes 786436
  70.6 5.6 %copy-start.8 = (bf16[1024,512]{1,0:T(8,128)(2,1)S(1)}, bf16[1024,512]{1,0:T(8,128)(2,1)}, u32[]{:S(2)}) copy-start(bf16[1024,512]{1,0:T(8,128)(2,1)} %all-gather.6.cloned.1.call-done) | copy-start | bytes 3145732
  76.0 1.0 copy-start.2
  76.0 29.7 %copy-start.3 = (bf16[512,1024]{1,0:T(8,128)(2,1)S(1)}, bf16[512,1024]{1,0:T(8,128)(2,1)}, u32[]{:S(2)}) copy-start(bf16[512,1024]{1,0:T(8,128)(2,1)} %param.20) | copy-start | bytes 3145732
  76.0 29.7 %collective-permute-start.1 = (f32[512,512]{1,0:T(8,128)S(1)}, f32[512,512]{1,0:T(8,128)S(1)}, u32[]{:S(2)}, u32[]{:S(2)}) collective-permute-start(f32[512,512]{1,0:T(8,128)S(1)} %convolution_bitcast_fusion), channel_id=1, source_target_pairs={{30,0},{0,2},{2,4},{4,6},{6,8},{8,10},{10,12},{12,14},{14,16},{16,... | collective-permute-start | bytes 3145736 | tf_op jit(solution)/shard_map/ppermute | solution.py:12
  77.3 29.2 %copy-start.9 = (s32[1,128]{1,0:T(1,128)S(1)}, s32[1,128]{1,0:T(1,128)}, u32[]{:S(2)}) copy-start(s32[1,128]{1,0:T(1,128)} %param.25) | copy-start | bytes 1540
  77.3 29.3 %copy-start.7 = (s32[1,4,128]{2,1,0:T(4,128)S(1)}, s32[1,4,128]{2,1,0:T(4,128)}, u32[]{:S(2)}) copy-start(s32[1,4,128]{2,1,0:T(4,128)} %param.26) | copy-start | bytes 6148
  106.4 7.4 %copy-start.1 = (f32[512,512]{1,0:T(8,128)}, f32[512,512]{1,0:T(8,128)S(1)}, u32[]{:S(2)}) copy-start(f32[512,512]{1,0:T(8,128)S(1)} %fusion.1) | copy-start | bytes 3145732
  106.4 2.7 %collective-permute-start.2 = (f32[512,512]{1,0:T(8,128)S(1)}, f32[512,512]{1,0:T(8,128)S(1)}, u32[]{:S(2)}, u32[]{:S(2)}) collective-permute-start(f32[512,512]{1,0:T(8,128)S(1)} %fusion.1), channel_id=1, source_target_pairs={{0,1},{1,0},{2,3},{3,2},{4,5},{5,4},{6,7},{7,6},{8,9},{9,8},{10,11... | collective-permute-start | bytes 3145736 | tf_op jit(solution)/shard_map/ppermute | solution.py:39
  113.3 26.3 %collective-permute-start.3 = (f32[128,512]{1,0:T(8,128)S(1)}, f32[128,512]{1,0:T(8,128)S(1)}, u32[]{:S(2)}, u32[]{:S(2)}) collective-permute-start(f32[128,512]{1,0:T(8,128)S(1)} %broadcast_select_fusion.3), channel_id=1, source_target_pairs={{0,2},{2,0},{1,3},{3,1},{4,6},{6,4},{5,7},{7,5},{8,10},{10,8},{9,1... | collective-permute-start | bytes 786440 | tf_op jit(solution)/shard_map/ppermute | solution.py:39
  141.5 23.8 %collective-permute-start.4 = (f32[128,512]{1,0:T(8,128)S(1)}, f32[128,512]{1,0:T(8,128)S(1)}, u32[]{:S(2)}, u32[]{:S(2)}) collective-permute-start(f32[128,512]{1,0:T(8,128)S(1)} %broadcast_select_fusion.2), channel_id=1, source_target_pairs={{0,4},{4,0},{1,5},{5,1},{2,6},{6,2},{3,7},{7,3},{8,12},{12,8},{9,1... | collective-permute-start | bytes 786440 | tf_op jit(solution)/shard_map/ppermute | solution.py:39
  167.4 24.0 %collective-permute-start.5 = (f32[128,512]{1,0:T(8,128)S(1)}, f32[128,512]{1,0:T(8,128)S(1)}, u32[]{:S(2)}, u32[]{:S(2)}) collective-permute-start(f32[128,512]{1,0:T(8,128)S(1)} %broadcast_select_fusion.1), channel_id=1, source_target_pairs={{0,8},{8,0},{1,9},{9,1},{2,10},{10,2},{3,11},{11,3},{4,12},{12,4},... | collective-permute-start | bytes 786440 | tf_op jit(solution)/shard_map/ppermute | solution.py:39
  193.4 27.0 %collective-permute-start.6 = (f32[128,512]{1,0:T(8,128)S(1)}, f32[128,512]{1,0:T(8,128)S(1)}, u32[]{:S(2)}, u32[]{:S(2)}) collective-permute-start(f32[128,512]{1,0:T(8,128)S(1)} %broadcast_select_fusion), channel_id=1, source_target_pairs={{0,16},{16,0},{1,17},{17,1},{2,18},{18,2},{3,19},{19,3},{4,20},{20... | collective-permute-start | bytes 786440 | tf_op jit(solution)/shard_map/ppermute | solution.py:39
Sparse Core Ops, SparseCore 0:
  9.6 11.7 all-gather.5
  52.1 9.6 reduce-scatter.1
where the time goes:
time: 259 us; the launch traced here: 254 us
  other arithmetic  127 us (49%)
  waiting for transfers between devices  66.6 us (26%)
  matrix products  17.8 us (7%)
  between operations  15.1 us (6%)
  blocking collectives  10.3 us (4%)
  starting transfers between devices  9.45 us (4%)
  local copies, waits for them, and re-layouts  7.82 us (3%)
    another operation x15, other arithmetic, interp_rows(): factor = jnp.linalg.cholesky(gram_matrix)  62.3 us
    another operation x10, other arithmetic, interp_rows(): return jax.scipy.linalg.cho_solve((factor, True), cross_term).T  52.7 us
    ppermute x2, waiting for transfers between devices, shifted(): return lax.ppermute(block, axis, route)  50.1 us
    all_gather x1, waiting for transfers between devices, per_device(): whole_group = lax.all_gather(sketch, 'blk', axis=0, tiled=True)  13.4 us
    another operation x2, other arithmetic, per_device(): jax.scipy.linalg.solve_triangular(diag_block, solved - back_prefix[1], lo...  9.82 us
    all_gather x4, blocking collectives, carried_in(): pieces = jax.tree.map(lambda part: lax.all_gather(part, axis), value)  8.28 us
    ppermute x2, starting transfers between devices, shifted(): return lax.ppermute(block, axis, route)  5.64 us
  transfers between devices with their start and end apart: 9, of which 4 were waited for; matrix products, arithmetic and copies ran while one was open for 43% of the time, Pallas kernels for 0%

commit v1 on v0

v1 whole, which is shorter than its diff:
```python
import functools

import jax
import jax.numpy as jnp
from jax import lax
from jax.experimental import pallas as pl
from jax.experimental.pallas import tpu as pltpu
from jax.sharding import PartitionSpec as P

highest = lax.Precision.HIGHEST
f32 = jnp.float32
contract_rows = (((0,), (0,)), ((), ()))
contract_cols = (((1,), (1,)), ((), ()))
VMEM_SPEC = pl.BlockSpec(memory_space=pltpu.VMEM)
SMEM_SPEC = pl.BlockSpec(memory_space=pltpu.SMEM)


def shifted(block, axis, distance):
    count = lax.axis_size(axis)
    return lax.ppermute(block, axis, [((i - distance) % count, i) for i in range(count)])


def from_partner(block, axis, apart):
    count = lax.axis_size(axis)
    return lax.ppermute(block, axis, [(i, i ^ 1 << apart) for i in range(count)])


def gathered(block):
    if lax.axis_size("blk") != 2:
        return lax.all_gather(block, "blk", axis=0, tiled=True)
    other = from_partner(block, "blk", 0)
    first = lax.axis_index("blk") == 0
    return jnp.concatenate(
        [jnp.where(first, block, other), jnp.where(first, other, block)], axis=0
    )


def invert_in_place(refs):
    size = refs[0].shape[-1]
    lane = lax.broadcasted_iota(jnp.int32, (1, size), 1)
    for k in range(0, size, 2):
        at0, at1 = lane == k, lane == k + 1
        pivot_cols = at0 | at1
        for ref in refs:
            value = ref[...]
            r0, r1 = value[k : k + 1, :], value[k + 1 : k + 2, :]
            p00, p01 = r0[:, k : k + 1], r0[:, k + 1 : k + 2]
            p10, p11 = r1[:, k : k + 1], r1[:, k + 1 : k + 2]
            q0 = 1.0 / p00
            ratio = p10 * q0
            q1 = 1.0 / (p11 - ratio * p01)
            r0 = jnp.where(pivot_cols, jnp.where(at0, 1.0, 0.0), r0)
            r1 = jnp.where(pivot_cols, jnp.where(at1, 1.0, 0.0), r1)
            new1 = (r1 - ratio * r0) * q1
            new0 = (r0 - p01 * new1) * q0
            ref[...] = (
                jnp.where(pivot_cols, 0.0, value)
                - value[:, k : k + 1] * new0
                - value[:, k + 1 : k + 2] * new1
            )
            ref[k : k + 1, :] = new0
            ref[k + 1 : k + 2, :] = new1


def factor_kernel(diag_ref, sub_ref, out_ref, *work):
    size = diag_ref.shape[1]
    blocks = diag_ref.shape[0] // size
    row = lax.broadcasted_iota(jnp.int32, (size, size), 0)
    col = lax.broadcasted_iota(jnp.int32, (size, size), 1)
    for k in range(blocks):
        work[k][...] = jnp.where(row >= col, diag_ref[k * size : (k + 1) * size, :], 0.0)
    invert_in_place(work)
    out_ref[...] = jnp.zeros_like(out_ref)
    for k in range(blocks):
        rows = slice(k * size, (k + 1) * size)
        inverse = work[k][...]
        out_ref[rows, rows] = inverse
        if k:
            step = jnp.dot(inverse, sub_ref[rows, :], precision=highest)
            before = out_ref[(k - 1) * size : k * size, : k * size]
            out_ref[rows, : k * size] = -jnp.dot(step, before, precision=highest)


def factor_inverse(diag, sub):
    total, size = diag.shape
    return pl.pallas_call(
        factor_kernel,
        out_shape=jax.ShapeDtypeStruct((total, total), f32),
        in_specs=[VMEM_SPEC] * 2,
        out_specs=VMEM_SPEC,
        scratch_shapes=[pltpu.VMEM((size, size), f32)] * (total // size),
        cost_estimate=pl.CostEstimate(flops=4 * 10**9, bytes_accessed=10**6, transcendentals=0),
        name="factor_inverse",
    )(diag, sub)


def pick_kernel(index_ref, low_ref, source_ref, out_ref):
    rows = source_ref.shape[0]
    low = low_ref[0]

    def body(i, _):
        for u in range(8):
            at = i * 8 + u
            local = index_ref[at] - low
            inside = (local >= 0) & (local < rows)
            line = source_ref[pl.ds(jnp.clip(local, 0, rows - 1), 1), :]
            out_ref[pl.ds(at, 1), :] = jnp.where(inside, line, 0.0)
        return 0

    lax.fori_loop(0, index_ref.shape[0] // 8, body, 0)


def pick(index, low, source):
    return pl.pallas_call(
        pick_kernel,
        out_shape=jax.ShapeDtypeStruct((index.shape[0], source.shape[1]), f32),
        in_specs=[SMEM_SPEC, SMEM_SPEC, VMEM_SPEC],
        out_specs=VMEM_SPEC,
        cost_estimate=pl.CostEstimate(flops=10**8, bytes_accessed=10**6, transcendentals=0),
        name="pick_rows",
    )(index, low.reshape(1), source)


def pick2_kernel(index_ref, own_ref, sib_ref, out_ref):
    half = own_ref.shape[0]

    def body(i, _):
        for u in range(8):
            at = i * 8 + u
            local = index_ref[at]
            inside = local < half
            spot = jnp.where(inside, local, local - half)
            out_ref[pl.ds(at, 1), :] = jnp.where(
                inside, own_ref[pl.ds(spot, 1), :], sib_ref[pl.ds(spot, 1), :]
            )
        return 0

    lax.fori_loop(0, index_ref.shape[0] // 8, body, 0)


def pick2(index, own, sib):
    return pl.pallas_call(
        pick2_kernel,
        out_shape=jax.ShapeDtypeStruct(own.shape, f32),
        in_specs=[SMEM_SPEC, VMEM_SPEC, VMEM_SPEC],
        out_specs=VMEM_SPEC,
        cost_estimate=pl.CostEstimate(flops=10**8, bytes_accessed=10**6, transcendentals=0),
        name="pick_merged",
    )(index, own, sib)


def interp_kernel(
    levels, index_ref, upper_ref, gram_ref, cross_ref, mine_ref, other_ref,
    leaf_out, merge_out, total_ref, *work,
):
    size = gram_ref.shape[0]
    work[0][...] = gram_ref[...]
    for j in range(levels):
        total_ref[j] = mine_ref[j] + other_ref[j]

        def body(i, _):
            for u in range(8):
                at = i * 8 + u
                work[j + 1][pl.ds(at, 1), :] = total_ref[j, pl.ds(index_ref[j, at], 1), :]
            return 0

        lax.fori_loop(0, size // 8, body, 0)
    invert_in_place(work)
    leaf_out[...] = jnp.dot(
        cross_ref[...], work[0][...], precision=highest, preferred_element_type=f32
    )
    for j in range(levels):
        rows = jnp.dot(
            total_ref[j], work[j + 1][...], precision=highest, preferred_element_type=f32
        )
        start = pl.multiple_of(upper_ref[j] * size, size)
        merge_out[j, pl.ds(start, size), :] = rows[:size]
        merge_out[j, pl.ds(pl.multiple_of(size - start, size), size), :] = rows[size:]


def interps(index, upper, gram, cross, mine, other):
    levels = index.shape[0]
    size = gram.shape[0]
    return pl.pallas_call(
        functools.partial(interp_kernel, levels),
        out_shape=(
            jax.ShapeDtypeStruct(cross.shape, f32),
            jax.ShapeDtypeStruct(mine.shape, f32),
        ),
        in_specs=[SMEM_SPEC, SMEM_SPEC] + [VMEM_SPEC] * 4,
        out_specs=(VMEM_SPEC, VMEM_SPEC),
        scratch_shapes=[pltpu.VMEM(mine.shape, f32)]
        + [pltpu.VMEM((size, size), f32)] * (levels + 1),
        cost_estimate=pl.CostEstimate(flops=4 * 10**9, bytes_accessed=10**6, transcendentals=0),
        name="interps",
    )(index, upper, gram, cross, mine, other)


def bf16_dot(left, right):
    return jnp.dot(left, right, preferred_element_type=f32)


def per_device(
    sketch,
    near_block,
    next_block,
    link_own,
    link_next,
    diag_block,
    sub_block,
    leaf_skeleton,
    merge_skeleton,
):
    rows = sketch.shape[0]
    blk_count = lax.axis_size("blk")
    blk = lax.axis_index("blk")
    leaf = lax.axis_index("leaf")
    following_half = shifted(sketch, "leaf", -1)
    previous_link = shifted(link_next, "leaf", 1)
    whole_group = gathered(sketch)
    diag_all, sub_all = gathered(diag_block), gathered(sub_block)
    links = gathered(jnp.concatenate([link_own, link_next], axis=0)[None])
    inter = link_own.shape[0]
    full_own = jnp.concatenate([links[i, :inter] for i in range(blk_count)], axis=1)
    full_next = jnp.concatenate([links[i, inter:] for i in range(blk_count)], axis=1)
    inverse = factor_inverse(diag_all, sub_all)
    near_part = bf16_dot(near_block, whole_group)
    load_part = bf16_dot(full_own, whole_group)
    following_group = gathered(following_half)
    load = load_part + bf16_dot(full_next, following_group)
    solved = jnp.dot(inverse, load, precision=highest)
    weights = lax.dot_general(inverse, solved, contract_rows, precision=highest).astype(
        jnp.bfloat16
    )
    part = inter // blk_count
    my_weights = lax.dynamic_slice_in_dim(weights, blk * part, part, 0)
    previous_half = shifted(my_weights, "leaf", 1)
    previous_weights = gathered(previous_half)
    direct = near_part + bf16_dot(next_block, following_group)
    own_back = lax.dot_general(link_own, weights, contract_rows, preferred_element_type=f32)
    from_previous = lax.dot_general(
        previous_link, previous_weights, contract_rows, preferred_element_type=f32
    )
    samples = direct - own_back - from_previous
    contrib = pick(leaf_skeleton[0], blk * rows, samples)
    chosen = contrib + from_partner(contrib, "blk", 0)
    leaf_cross = lax.dot_general(samples, chosen, contract_cols, precision=highest)
    leaf_gram = lax.dot_general(chosen, chosen, contract_cols, precision=highest)
    width = chosen.shape[1] // blk_count
    current = lax.dynamic_slice_in_dim(chosen, blk * width, width, 1)
    rank = chosen.shape[0]
    levels = merge_skeleton.shape[1]
    upper = (leaf >> jnp.arange(levels, dtype=jnp.int32)) & 1
    local_sets = (merge_skeleton[0] + rank * upper[:, None]) % (2 * rank)
    crosses = []
    for j in range(levels):
        sibling = from_partner(current, "leaf", j)
        picked = pick2(local_sets[j], current, sibling)
        crosses.append(
            lax.dot_general(
                jnp.concatenate([current, sibling], axis=0), picked, contract_cols,
                precision=highest,
            )
        )
        current = picked
    mine = jnp.stack(crosses, axis=0)
    other = from_partner(mine, "blk", 0)
    leaf_interp, merge_interp = interps(
        local_sets, upper, leaf_gram, leaf_cross, mine, other
    )
    return (samples, leaf_interp, merge_interp[None])


def solution(mesh):
    both = ("leaf", "blk")
    placed = (
        P(both, None),
        P(both, None),
        P(both, None),
        P("leaf", "blk"),
        P("leaf", "blk"),
        P(both, None),
        P(both, None),
        P("leaf", None),
        P("leaf", None, None),
    )
    return jax.shard_map(
        per_device,
        mesh=mesh,
        in_specs=placed,
        out_specs=(P(both, None), P(both, None), P(both, None, None, None)),
        check_vma=False,
    )
```

time: 259 us -> 124 us (0.48); the launches traced: 254 us -> 124 us
  other arithmetic: 127 us -> 5.33 us
  Pallas kernels: 0 us -> 60.3 us
  waiting for transfers between devices: 66.6 us -> 29.3 us
  between operations: 15.1 us -> 0.95 us
  blocking collectives: 10.3 us -> 0 us
  matrix products: 17.8 us -> 13.5 us
    another operation x27 -> x1, other arithmetic: 125 us -> 0.05 us  [per_device(): mine = jnp.stack(crosses, axis=0)]
    pallas_call x0 -> x7, Pallas kernels: none -> 60.3 us  [the longest x1 30.4 us: interps(): pl.pallas_call(functools.partial(interp_kernel, levels), out_shape=(jax.S...]
    ppermute x7 -> x15, waiting for transfers between devices: 52.5 us -> 29.3 us  [the longest x12 20.6 us: from_partner(): lax.ppermute(block, axis, [(i, i ^ 1 << apart) for i in range(count)])]
    all_gather x1 -> x0, waiting for transfers between devices: 13.4 us -> none  [per_device(): whole_group = lax.all_gather(sketch, 'blk', axis=0, tiled=True)]
    all_gather x5 -> x0, blocking collectives: 10.3 us -> none  [the longest x4 8.28 us: carried_in(): pieces = jax.tree.map(lambda part: lax.all_gather(part, axis), value)]
    gather x5 -> x0, local copies, waits for them, and re-layouts: 5.49 us -> none  [the longest x4 3.03 us: per_device(): chosen = jnp.take(candidates, own_sets[level_index], axis=0)]
    another operation x13 -> x0, matrix products: 5.09 us -> none  [the longest x10 3.07 us: interp_rows(): return jax.scipy.linalg.cho_solve((factor, True), cross_term).T]
    unnamed x22 -> x42, local copies, waits for them, and re-layouts: 1.89 us -> 4.94 us
  transfers between devices with their start and end apart: 9 -> 15, of which waited for: 4 -> 7; matrix products, arithmetic and copies ran while one was open for 43% -> 12% of each run, Pallas kernels for 0% -> 15%
where the time goes in v1:
time: 124 us
  Pallas kernels  60.3 us (49%)
  waiting for transfers between devices  29.3 us (24%)
  matrix products  13.5 us (11%)
  starting transfers between devices  8.85 us (7%)
  local copies, waits for them, and re-layouts  5.64 us (5%)
  other arithmetic  5.33 us (4%)
    pallas_call x1, Pallas kernels, interps(): pl.pallas_call(functools.partial(interp_kernel, levels), out_shape=(jax.S...  30.4 us
    ppermute x12, waiting for transfers between devices, from_partner(): lax.ppermute(block, axis, [(i, i ^ 1 << apart) for i in range(count)])  20.6 us
    pallas_call x1, Pallas kernels, factor_inverse(): pl.pallas_call(factor_kernel, out_shape=jax.ShapeDtypeStruct((total, tota...  18.1 us
    pallas_call x4, Pallas kernels, pick2(): pl.pallas_call(pick2_kernel, out_shape=jax.ShapeDtypeStruct(own.shape, f3...  9.16 us
    ppermute x3, waiting for transfers between devices, shifted(): lax.ppermute(block, axis, [((i - distance) % count, i) for i in range(cou...  8.68 us
    ppermute x3, starting transfers between devices, shifted(): lax.ppermute(block, axis, [((i - distance) % count, i) for i in range(cou...  6.78 us
    dot_general x4, matrix products, per_device(): lax.dot_general(jnp.concatenate([current, sibling], axis=0), picked, cont...  5.6 us
    unnamed x42, local copies, waits for them, and re-layouts  4.94 us
  transfers between devices with their start and end apart: 15, of which 7 were waited for; matrix products, arithmetic and copies ran while one was open for 12% of the time, Pallas kernels for 15%

profile of v1, /device:TPU:0, one launch (start us, length us, event | category | flops | bytes accessed | tf_op | source)
XLA Modules:
  0.0 123.8 jit_solution(10528202033292222462)
XLA Ops:
  1.2 6.5 %collective-permute-start.1 = (bf16[512,512]{1,0:T(8,128)(2,1)}, bf16[512,512]{1,0:T(8,128)(2,1)S(1)}, u32[]{:S(2)}, u32[]{:S(2)}) collective-permute-start(bf16[512,512]{1,0:T(8,128)(2,1)} %param.9), channel_id=1, source_target_pairs={{2,0},{4,2},{6,4},{8,6},{10,8},{12,10},{14,12},{16,14},{18,16},{20... | collective-permute-start | bytes 1572872 | tf_op jit(solution)/shard_map/ppermute | solution.py:20
  8.3 1.9 %maximum_bitcast_fusion = bf16[1,512,512]{2,1,0:T(8,128)(2,1)} fusion(bf16[256,512]{1,0:T(8,128)(2,1)} %param.13, bf16[256,512]{1,0:T(8,128)(2,1)} %param.12), kind=kLoop, calls=%fused_computation.13 | loop fusion | flops 1048576 | bytes 1048576 | tf_op jit(solution)/shard_map/broadcast_in_dim | solution.py:222
  11.7 18.1 %factor_inverse.1 = f32[256,256]{1,0:T(8,128)} custom-call(f32[256,128]{1,0:T(8,128)} %pad_maximum_fusion.7.diag_ref, f32[256,128]{1,0:T(8,128)} %pad_maximum_fusion.8.sub_ref), custom_call_target="tpu_custom_call" | custom-call | flops 4000000000 | bytes 1000000 | tf_op jit(solution)/shard_map/factor_inverse/pallas_call | solution.py:86
  35.1 8.7 %collective-permute-done.6 = bf16[128,512]{1,0:T(8,128)(2,1)S(1)} collective-permute-done((bf16[128,512]{1,0:T(8,128)(2,1)S(1)}, bf16[128,512]{1,0:T(8,128)(2,1)S(1)}, u32[]{:S(2)}, u32[]{:S(2)}) %collective-permute-start.6) | collective-permute-done | bytes 131104 | tf_op jit(solution)/shard_map/ppermute | solution.py:20
  44.2 1.0 collective-permute-done.7
  45.6 1.7 %fusion.1 = f32[512,512]{0,1:T(8,128)} fusion(f32[512,512]{0,1:T(8,128)S(1)} %fusion.10, f32[512,512]{0,1:T(8,128)S(1)} %fusion.37, f32[512,512]{0,1:T(8,128)S(1)} %fusion.3, bf16[512,1024]{1,0:T(8,128)(2,1)S(1)} %copy-done.9, bf16[512,512]{1,0:T(8,128)(2,1)S(1)} %get-tuple-element.8, bf16[512,512]{1,0:T(8,128)(2,1)S(1)} %get-tuple-element.7), kind=kOutput, calls=%fused_computation.2 | convolution fusion | flops 539754496 | bytes 6291456 | tf_op jit(solution)/shard_map/dot_general | solution.py:200
  47.2 2.8 %pick_rows.1 = f32[128,512]{1,0:T(8,128)} custom-call(s32[128]{0:T(128)} %bitcast.59, s32[1]{0:T(128)} %bitcast.8.low_ref, f32[512,512]{1,0:T(8,128)} %bitcast.57), custom_call_target="tpu_custom_call" | custom-call | flops 100000000 | bytes 1000000 | tf_op jit(solution)/shard_map/pick_rows/pallas_call | solution.py:114
  50.4 1.3 %collective-permute-done.9 = f32[128,512]{1,0:T(8,128)S(1)} collective-permute-done((f32[128,512]{1,0:T(8,128)}, f32[128,512]{1,0:T(8,128)S(1)}, u32[]{:S(2)}, u32[]{:S(2)}) %collective-permute-start.9) | collective-permute-done | bytes 262176 | tf_op jit(solution)/shard_map/ppermute | solution.py:25
  51.8 1.0 add.36
  53.5 5.1 %collective-permute-done.10.sib_ref = f32[128,256]{1,0:T(8,128)S(1)} collective-permute-done((f32[128,256]{1,0:T(8,128)S(1)}, f32[128,256]{1,0:T(8,128)S(1)}, u32[]{:S(2)}, u32[]{:S(2)}) %collective-permute-start.10) | collective-permute-done | bytes 131104 | tf_op jit(solution)/shard_map/ppermute | solution.py:25
  59.2 2.3 %pick_merged.4.own_ref = f32[128,256]{1,0:T(8,128)} custom-call(s32[128]{0:T(128)} %get-tuple-element.23.index_ref, f32[128,256]{1,0:T(8,128)} %copy-done.6, f32[128,256]{1,0:T(8,128)} %copy-done.12), custom_call_target="tpu_custom_call" | custom-call | flops 100000000 | bytes 1000000 | tf_op jit(solution)/shard_map/pick_merged/pallas_call | solution.py:142
  61.5 5.2 %collective-permute-done.11.sib_ref = f32[128,256]{1,0:T(8,128)S(1)} collective-permute-done((f32[128,256]{1,0:T(8,128)}, f32[128,256]{1,0:T(8,128)S(1)}, u32[]{:S(2)}, u32[]{:S(2)}) %collective-permute-start.11) | collective-permute-done | bytes 131104 | tf_op jit(solution)/shard_map/ppermute | solution.py:25
  67.4 2.3 %pick_merged.5.own_ref = f32[128,256]{1,0:T(8,128)} custom-call(s32[128]{0:T(128)} %get-tuple-element.26.index_ref, f32[128,256]{1,0:T(8,128)} %pick_merged.4.own_ref, f32[128,256]{1,0:T(8,128)} %copy-done.13), custom_call_target="tpu_custom_call" | custom-call | flops 100000000 | bytes 1000000 | tf_op jit(solution)/shard_map/pick_merged/pallas_call | solution.py:142
  69.7 1.4 %convolution_bitcast_fusion.3 = f32[1,256,128]{2,1,0:T(8,128)S(1)} fusion(f32[128,256]{1,0:T(8,128)} %pick_merged.4.own_ref, f32[128,256]{1,0:T(8,128)} %copy-done.12, f32[128,256]{1,0:T(8,128)} %copy-done.6), kind=kOutput, calls=%fused_computation.8 | convolution fusion | flops 100728832 | bytes 524288 | tf_op jit(solution)/shard_map/dot_general | solution.py:260
  71.1 3.7 %collective-permute-done.12.sib_ref = f32[128,256]{1,0:T(8,128)S(1)} collective-permute-done((f32[128,256]{1,0:T(8,128)}, f32[128,256]{1,0:T(8,128)S(1)}, u32[]{:S(2)}, u32[]{:S(2)}) %collective-permute-start.12) | collective-permute-done | bytes 131104 | tf_op jit(solution)/shard_map/ppermute | solution.py:25
  75.5 2.3 %pick_merged.6.own_ref = f32[128,256]{1,0:T(8,128)} custom-call(s32[128]{0:T(128)} %get-tuple-element.25.index_ref, f32[128,256]{1,0:T(8,128)} %pick_merged.5.own_ref, f32[128,256]{1,0:T(8,128)} %copy-done.14), custom_call_target="tpu_custom_call" | custom-call | flops 100000000 | bytes 1000000 | tf_op jit(solution)/shard_map/pick_merged/pallas_call | solution.py:142
  77.8 1.4 %convolution_bitcast_fusion.2 = f32[1,256,128]{2,1,0:T(8,128)S(1)} fusion(f32[128,256]{1,0:T(8,128)} %pick_merged.5.own_ref, f32[128,256]{1,0:T(8,128)} %copy-done.13, f32[128,256]{1,0:T(8,128)S(1)} %copy-done.3), kind=kOutput, calls=%fused_computation.7 | convolution fusion | flops 100728832 | bytes 524288 | tf_op jit(solution)/shard_map/dot_general | solution.py:260
  79.2 1.3 %convolution_bitcast_fusion.1 = f32[1,256,128]{2,1,0:T(8,128)S(1)} fusion(f32[128,256]{1,0:T(8,128)} %pick_merged.6.own_ref, f32[128,256]{1,0:T(8,128)} %copy-done.14, f32[128,256]{1,0:T(8,128)S(1)} %copy-done.4), kind=kOutput, calls=%fused_computation.6 | convolution fusion | flops 100728832 | bytes 524288 | tf_op jit(solution)/shard_map/dot_general | solution.py:260
  80.5 4.2 %collective-permute-done.13.sib_ref = f32[128,256]{1,0:T(8,128)S(1)} collective-permute-done((f32[128,256]{1,0:T(8,128)}, f32[128,256]{1,0:T(8,128)S(1)}, u32[]{:S(2)}, u32[]{:S(2)}) %collective-permute-start.13) | collective-permute-done | bytes 131104 | tf_op jit(solution)/shard_map/ppermute | solution.py:25
  85.4 2.3 %pick_merged.7 = f32[128,256]{1,0:T(8,128)} custom-call(s32[128]{0:T(128)} %get-tuple-element.24.index_ref, f32[128,256]{1,0:T(8,128)} %pick_merged.6.own_ref, f32[128,256]{1,0:T(8,128)} %copy-done.15), custom_call_target="tpu_custom_call" | custom-call | flops 100000000 | bytes 1000000 | tf_op jit(solution)/shard_map/pick_merged/pallas_call | solution.py:142
  87.7 1.4 %convolution_bitcast_fusion = f32[1,256,128]{2,1,0:T(8,128)S(1)} fusion(f32[128,256]{1,0:T(8,128)} %pick_merged.7, f32[128,256]{1,0:T(8,128)} %copy-done.15, f32[128,256]{1,0:T(8,128)S(1)} %copy-done.5), kind=kOutput, calls=%fused_computation.5 | convolution fusion | flops 100728832 | bytes 524288 | tf_op jit(solution)/shard_map/dot_general | solution.py:260
  89.9 1.0 fusion.38.gram_ref
  90.9 1.7 %fusion.39.cross_ref = f32[512,128]{1,0:T(8,128)} fusion(f32[512,512]{0,1:T(8,128)S(1)} %copy-done.1, f32[128,512]{1,0:T(8,128)S(1)} %add.36), kind=kOutput, calls=%fused_computation.80 | convolution fusion | flops 402653184 | bytes 1572864 | tf_op jit(solution)/shard_map/dot_general | solution.py:247
  93.5 30.4 %interps.1 = (f32[512,128]{1,0:T(8,128)}, f32[4,256,128]{2,1,0:T(8,128)}) custom-call(s32[4,128]{1,0:T(4,128)} %copy-done.18, s32[4]{0:T(128)} %shift-right-arithmetic_and_fusion.upper_ref, f32[128,128]{1,0:T(8,128)} %fusion.38.gram_ref, f32[512,128]{1,0:T(8,128)} %fusion.39.cross_ref, f32[4,256,128]{2,1,0:T(8,128)} %copy-done.11, f32[4,256,128]{2,1,0:T(8,128)} %copy-done.20), custom_call_target="tpu_custom_call" | custom-call | flops 4000000000 | bytes 1000000 | tf_op jit(solution)/shard_map/interps/pallas_call | solution.py:184
  (86 shorter events, 14.0 us)
Async XLA Ops:
  0.6 33.8 %copy-start = (bf16[512,1024]{1,0:T(8,128)(2,1)S(1)}, bf16[512,1024]{1,0:T(8,128)(2,1)}, u32[]{:S(2)}) copy-start(bf16[512,1024]{1,0:T(8,128)(2,1)} %param.10) | copy-start | bytes 3145732
  0.6 9.7 %copy-start.17 = (f32[128,128]{1,0:T(8,128)S(1)}, f32[128,128]{1,0:T(8,128)}, u32[]{:S(2)}) copy-start(f32[128,128]{1,0:T(8,128)} %param.14) | copy-start | bytes 196612
  0.7 9.7 %copy-start.16 = (f32[128,128]{1,0:T(8,128)S(1)}, f32[128,128]{1,0:T(8,128)}, u32[]{:S(2)}) copy-start(f32[128,128]{1,0:T(8,128)} %param.15) | copy-start | bytes 196612
  0.7 29.7 %collective-permute-start = (bf16[512,512]{1,0:T(8,128)(2,1)}, bf16[512,512]{1,0:T(8,128)(2,1)S(1)}, u32[]{:S(2)}, u32[]{:S(2)}) collective-permute-start(bf16[512,512]{1,0:T(8,128)(2,1)} %param.9), channel_id=1, source_target_pairs={{0,1},{1,0},{2,3},{3,2},{4,5},{5,4},{6,7},{7,6},{8,9},{9,8},{10,11... | collective-permute-start | bytes 1572872 | tf_op jit(solution)/shard_map/ppermute | solution.py:25
  1.2 28.5 %collective-permute-start.1 = (bf16[512,512]{1,0:T(8,128)(2,1)}, bf16[512,512]{1,0:T(8,128)(2,1)S(1)}, u32[]{:S(2)}, u32[]{:S(2)}) collective-permute-start(bf16[512,512]{1,0:T(8,128)(2,1)} %param.9), channel_id=1, source_target_pairs={{2,0},{4,2},{6,4},{8,6},{10,8},{12,10},{14,12},{16,14},{18,16},{20... | collective-permute-start | bytes 1572872 | tf_op jit(solution)/shard_map/ppermute | solution.py:20
  7.8 2.4 %collective-permute-start.3 = (f32[128,128]{1,0:T(8,128)}, f32[128,128]{1,0:T(8,128)S(1)}, u32[]{:S(2)}, u32[]{:S(2)}) collective-permute-start(f32[128,128]{1,0:T(8,128)} %param.14), channel_id=1, source_target_pairs={{0,1},{1,0},{2,3},{3,2},{4,5},{5,4},{6,7},{7,6},{8,9},{9,8},{10,11... | collective-permute-start | bytes 196616 | tf_op jit(solution)/shard_map/ppermute | solution.py:25
  7.9 2.4 %collective-permute-start.4 = (f32[128,128]{1,0:T(8,128)}, f32[128,128]{1,0:T(8,128)S(1)}, u32[]{:S(2)}, u32[]{:S(2)}) collective-permute-start(f32[128,128]{1,0:T(8,128)} %param.15), channel_id=1, source_target_pairs={{0,1},{1,0},{2,3},{3,2},{4,5},{5,4},{6,7},{7,6},{8,9},{9,8},{10,11... | collective-permute-start | bytes 196616 | tf_op jit(solution)/shard_map/ppermute | solution.py:25
  8.3 36.9 %collective-permute-start.8 = (bf16[256,512]{1,0:T(8,128)(2,1)}, bf16[256,512]{1,0:T(8,128)(2,1)S(1)}, u32[]{:S(2)}, u32[]{:S(2)}) collective-permute-start(bf16[256,512]{1,0:T(8,128)(2,1)} %param.13), channel_id=1, source_target_pairs={{30,0},{0,2},{2,4},{4,6},{6,8},{8,10},{10,12},{12,14},{14,16},{16,... | collective-permute-start | bytes 786440 | tf_op jit(solution)/shard_map/ppermute | solution.py:20
  10.1 19.9 %collective-permute-start.5 = (bf16[1,512,512]{2,1,0:T(8,128)(2,1)}, bf16[1,512,512]{2,1,0:T(8,128)(2,1)S(1)}, u32[]{:S(2)}, u32[]{:S(2)}) collective-permute-start(bf16[1,512,512]{2,1,0:T(8,128)(2,1)} %maximum_bitcast_fusion), channel_id=1, source_target_pairs={{0,1},{1,0},{2,3},{3,2},{4,5},{5,4},{6,7},{7,6},{8,9},{9,8},{10,11... | collective-permute-start | bytes 1572872 | tf_op jit(solution)/shard_map/ppermute | solution.py:25
  11.7 18.4 %copy-start.2 = (bf16[256,512]{1,0:T(8,128)(2,1)S(1)}, bf16[256,512]{1,0:T(8,128)(2,1)}, u32[]{:S(2)}) copy-start(bf16[256,512]{1,0:T(8,128)(2,1)} %param.12) | copy-start | bytes 786436
  11.7 18.4 %copy-start.7 = (bf16[256,512]{1,0:T(8,128)(2,1)S(1)}, bf16[256,512]{1,0:T(8,128)(2,1)}, u32[]{:S(2)}) copy-start(bf16[256,512]{1,0:T(8,128)(2,1)} %param.13) | copy-start | bytes 786436
  29.7 2.1 %collective-permute-start.2 = (bf16[512,512]{1,0:T(8,128)(2,1)S(1)}, bf16[512,512]{1,0:T(8,128)(2,1)S(1)}, u32[]{:S(2)}, u32[]{:S(2)}) collective-permute-start(bf16[512,512]{1,0:T(8,128)(2,1)S(1)} %collective-permute-done.1), channel_id=1, source_target_pairs={{0,1},{1,0},{2,3},{3,2},{4,5},{5,4},{6,7},{7,6},{8,9},{9,8},{10,11... | collective-permute-start | bytes 1572872 | tf_op jit(solution)/shard_map/ppermute | solution.py:25
  34.2 9.6 %collective-permute-start.6 = (bf16[128,512]{1,0:T(8,128)(2,1)S(1)}, bf16[128,512]{1,0:T(8,128)(2,1)S(1)}, u32[]{:S(2)}, u32[]{:S(2)}) collective-permute-start(bf16[128,512]{1,0:T(8,128)(2,1)S(1)} %constant_dynamic-slice_fusion.1), channel_id=1, source_target_pairs={{30,0},{0,2},{2,4},{4,6},{6,8},{8,10},{10,12},{12,14},{14,16},{16,... | collective-permute-start | bytes 393224 | tf_op jit(solution)/shard_map/ppermute | solution.py:20
  43.8 1.3 %collective-permute-start.7 = (bf16[128,512]{1,0:T(8,128)(2,1)S(1)}, bf16[128,512]{1,0:T(8,128)(2,1)S(1)}, u32[]{:S(2)}, u32[]{:S(2)}) collective-permute-start(bf16[128,512]{1,0:T(8,128)(2,1)S(1)} %collective-permute-done.6), channel_id=1, source_target_pairs={{0,1},{1,0},{2,3},{3,2},{4,5},{5,4},{6,7},{7,6},{8,9},{9,8},{10,11... | collective-permute-start | bytes 393224 | tf_op jit(solution)/shard_map/ppermute | solution.py:25
  50.0 1.7 %collective-permute-start.9 = (f32[128,512]{1,0:T(8,128)}, f32[128,512]{1,0:T(8,128)S(1)}, u32[]{:S(2)}, u32[]{:S(2)}) collective-permute-start(f32[128,512]{1,0:T(8,128)} %pick_rows.1), channel_id=1, source_target_pairs={{0,1},{1,0},{2,3},{3,2},{4,5},{5,4},{6,7},{7,6},{8,9},{9,8},{10,11... | collective-permute-start | bytes 786440 | tf_op jit(solution)/shard_map/ppermute | solution.py:25
  50.4 20.7 %copy-start.18 = (s32[4,128]{1,0:T(4,128)}, s32[4,128]{1,0:T(4,128)S(1)}, u32[]{:S(2)}) copy-start(s32[4,128]{1,0:T(4,128)S(1)} %add_select_fusion.index_ref) | copy-start | bytes 6148
  52.8 5.8 %collective-permute-start.10 = (f32[128,256]{1,0:T(8,128)S(1)}, f32[128,256]{1,0:T(8,128)S(1)}, u32[]{:S(2)}, u32[]{:S(2)}) collective-permute-start(f32[128,256]{1,0:T(8,128)S(1)} %constant_dynamic-slice_fusion.own_ref), channel_id=1, source_target_pairs={{0,2},{2,0},{4,6},{6,4},{8,10},{10,8},{12,14},{14,12},{16,18},{18,... | collective-permute-start | bytes 393224 | tf_op jit(solution)/shard_map/ppermute | solution.py:25
  61.5 16.3 %copy-start.3 = (f32[128,256]{1,0:T(8,128)S(1)}, f32[128,256]{1,0:T(8,128)}, u32[]{:S(2)}) copy-start(f32[128,256]{1,0:T(8,128)} %pick_merged.4.own_ref) | copy-start | bytes 393220
  61.5 5.2 %collective-permute-start.11 = (f32[128,256]{1,0:T(8,128)}, f32[128,256]{1,0:T(8,128)S(1)}, u32[]{:S(2)}, u32[]{:S(2)}) collective-permute-start(f32[128,256]{1,0:T(8,128)} %pick_merged.4.own_ref), channel_id=1, source_target_pairs={{0,4},{2,6},{4,0},{6,2},{8,12},{10,14},{12,8},{14,10},{16,20},{18,... | collective-permute-start | bytes 393224 | tf_op jit(solution)/shard_map/ppermute | solution.py:25
  69.6 9.5 %copy-start.4 = (f32[128,256]{1,0:T(8,128)S(1)}, f32[128,256]{1,0:T(8,128)}, u32[]{:S(2)}) copy-start(f32[128,256]{1,0:T(8,128)} %pick_merged.5.own_ref) | copy-start | bytes 393220
  69.6 5.2 %collective-permute-start.12 = (f32[128,256]{1,0:T(8,128)}, f32[128,256]{1,0:T(8,128)S(1)}, u32[]{:S(2)}, u32[]{:S(2)}) collective-permute-start(f32[128,256]{1,0:T(8,128)} %pick_merged.5.own_ref), channel_id=1, source_target_pairs={{0,8},{2,10},{4,12},{6,14},{8,0},{10,2},{12,4},{14,6},{16,24},{18,... | collective-permute-start | bytes 393224 | tf_op jit(solution)/shard_map/ppermute | solution.py:25
  77.8 9.9 %copy-start.5 = (f32[128,256]{1,0:T(8,128)S(1)}, f32[128,256]{1,0:T(8,128)}, u32[]{:S(2)}) copy-start(f32[128,256]{1,0:T(8,128)} %pick_merged.6.own_ref) | copy-start | bytes 393220
  77.8 7.0 %collective-permute-start.13 = (f32[128,256]{1,0:T(8,128)}, f32[128,256]{1,0:T(8,128)S(1)}, u32[]{:S(2)}, u32[]{:S(2)}) collective-permute-start(f32[128,256]{1,0:T(8,128)} %pick_merged.6.own_ref), channel_id=1, source_target_pairs={{0,16},{2,18},{4,20},{6,22},{8,24},{10,26},{12,28},{14,30},{16,0},... | collective-permute-start | bytes 393224 | tf_op jit(solution)/shard_map/ppermute | solution.py:25
  89.2 3.4 %collective-permute-start.14 = (f32[4,256,128]{2,1,0:T(8,128)S(1)}, f32[4,256,128]{2,1,0:T(8,128)S(1)}, u32[]{:S(2)}, u32[]{:S(2)}) collective-permute-start(f32[4,256,128]{2,1,0:T(8,128)S(1)} %pad_maximum_fusion.6.mine_ref), channel_id=1, source_target_pairs={{0,1},{1,0},{2,3},{3,2},{4,5},{5,4},{6,7},{7,6},{8,9},{9,8},{10,11... | collective-permute-start | bytes 1572872 | tf_op jit(solution)/shard_map/ppermute | solution.py:25
  (12 other events, 22.4 us)

commit v2 on v1

--- a/solution.py
+++ b/solution.py
@@ -35,31 +35,40 @@
     )
 
 
-def invert_in_place(refs):
+def invert_in_place(refs, block=32):
     size = refs[0].shape[-1]
+    block = min(block, size)
     lane = lax.broadcasted_iota(jnp.int32, (1, size), 1)
-    for k in range(0, size, 2):
-        at0, at1 = lane == k, lane == k + 1
-        pivot_cols = at0 | at1
+    row = lax.broadcasted_iota(jnp.int32, (size, 1), 0)
+    inner = lax.broadcasted_iota(jnp.int32, (block, 1), 0)
+    for s in range(0, size, block):
+        panels = [ref[s : s + block, :] for ref in refs]
+        for k in range(0, block, 2):
+            at0, at1 = lane == s + k, lane == s + k + 1
+            pivot_cols = at0 | at1
+            for i, panel in enumerate(panels):
+                col0 = jnp.broadcast_to(panel[:, s + k : s + k + 1], (block, size))
+                col1 = jnp.broadcast_to(panel[:, s + k + 1 : s + k + 2], (block, size))
+                r0, r1 = panel[k : k + 1, :], panel[k + 1 : k + 2, :]
+                p00, p10 = col0[k : k + 1, :], col0[k + 1 : k + 2, :]
+                p01, p11 = col1[k : k + 1, :], col1[k + 1 : k + 2, :]
+                q0 = 1.0 / p00
+                ratio = p10 * q0
+                q1 = 1.0 / (p11 - ratio * p01)
+                r0 = jnp.where(pivot_cols, jnp.where(at0, 1.0, 0.0), r0)
+                r1 = jnp.where(pivot_cols, jnp.where(at1, 1.0, 0.0), r1)
+                new1 = (r1 - ratio * r0) * q1
+                new0 = (r0 - p01 * new1) * q0
+                rest = jnp.where(pivot_cols, 0.0, panel) - col0 * new0 - col1 * new1
+                panels[i] = jnp.where(inner == k, new0, jnp.where(inner == k + 1, new1, rest))
+        outside = (lane >= s) & (lane < s + block) & ((row < s) | (row >= s + block))
+        for ref, panel in zip(refs, panels):
+            ref[s : s + block, :] = panel
         for ref in refs:
             value = ref[...]
-            r0, r1 = value[k : k + 1, :], value[k + 1 : k + 2, :]
-            p00, p01 = r0[:, k : k + 1], r0[:, k + 1 : k + 2]
-            p10, p11 = r1[:, k : k + 1], r1[:, k + 1 : k + 2]
-            q0 = 1.0 / p00
-            ratio = p10 * q0
-            q1 = 1.0 / (p11 - ratio * p01)
-            r0 = jnp.where(pivot_cols, jnp.where(at0, 1.0, 0.0), r0)
-            r1 = jnp.where(pivot_cols, jnp.where(at1, 1.0, 0.0), r1)
-            new1 = (r1 - ratio * r0) * q1
-            new0 = (r0 - p01 * new1) * q0
-            ref[...] = (
-                jnp.where(pivot_cols, 0.0, value)
-                - value[:, k : k + 1] * new0
-                - value[:, k + 1 : k + 2] * new1
+            ref[...] = jnp.where(outside, 0.0, value) - jnp.dot(
+                jnp.where(outside, value, 0.0), value, precision=highest
             )
-            ref[k : k + 1, :] = new0
-            ref[k + 1 : k + 2, :] = new1
 
 
 def factor_kernel(diag_ref, sub_ref, out_ref, *work):
@@ -94,59 +103,44 @@
     )(diag, sub)
 
 
+def one_hot(column, first, count):
+    spots = lax.broadcasted_iota(jnp.int32, (column.shape[0], count), 1) + first
+    return jnp.where(column == spots, 1.0, 0.0)
+
+
 def pick_kernel(index_ref, low_ref, source_ref, out_ref):
-    rows = source_ref.shape[0]
-    low = low_ref[0]
-
-    def body(i, _):
-        for u in range(8):
-            at = i * 8 + u
-            local = index_ref[at] - low
-            inside = (local >= 0) & (local < rows)
-            line = source_ref[pl.ds(jnp.clip(local, 0, rows - 1), 1), :]
-            out_ref[pl.ds(at, 1), :] = jnp.where(inside, line, 0.0)
-        return 0
-
-    lax.fori_loop(0, index_ref.shape[0] // 8, body, 0)
+    chosen = one_hot(index_ref[...], low_ref[0], source_ref.shape[0])
+    out_ref[...] = jnp.dot(chosen, source_ref[...], precision=highest)
 
 
 def pick(index, low, source):
     return pl.pallas_call(
         pick_kernel,
         out_shape=jax.ShapeDtypeStruct((index.shape[0], source.shape[1]), f32),
-        in_specs=[SMEM_SPEC, SMEM_SPEC, VMEM_SPEC],
+        in_specs=[VMEM_SPEC, SMEM_SPEC, VMEM_SPEC],
         out_specs=VMEM_SPEC,
         cost_estimate=pl.CostEstimate(flops=10**8, bytes_accessed=10**6, transcendentals=0),
         name="pick_rows",
-    )(index, low.reshape(1), source)
+    )(index[:, None], low.reshape(1), source)
 
 
 def pick2_kernel(index_ref, own_ref, sib_ref, out_ref):
     half = own_ref.shape[0]
-
-    def body(i, _):
-        for u in range(8):
-            at = i * 8 + u
-            local = index_ref[at]
-            inside = local < half
-            spot = jnp.where(inside, local, local - half)
-            out_ref[pl.ds(at, 1), :] = jnp.where(
-                inside, own_ref[pl.ds(spot, 1), :], sib_ref[pl.ds(spot, 1), :]
-            )
-        return 0
-
-    lax.fori_loop(0, index_ref.shape[0] // 8, body, 0)
+    index = index_ref[...]
+    out_ref[...] = jnp.dot(
+        one_hot(index, 0, half), own_ref[...], precision=highest
+    ) + jnp.dot(one_hot(index, half, half), sib_ref[...], precision=highest)
 
 
 def pick2(index, own, sib):
     return pl.pallas_call(
         pick2_kernel,
         out_shape=jax.ShapeDtypeStruct(own.shape, f32),
-        in_specs=[SMEM_SPEC, VMEM_SPEC, VMEM_SPEC],
+        in_specs=[VMEM_SPEC] * 3,
         out_specs=VMEM_SPEC,
         cost_estimate=pl.CostEstimate(flops=10**8, bytes_accessed=10**6, transcendentals=0),
         name="pick_merged",
-    )(index, own, sib)
+    )(index[:, None], own, sib)
 
 
 def interp_kernel(

time: 124 us -> 99.9 us (0.81)
  Pallas kernels: 60.3 us -> 34.6 us
  local copies, waits for them, and re-layouts: 5.64 us -> 9.39 us
  waiting for transfers between devices: 29.3 us -> 27.9 us
    pallas_call x1, Pallas kernels: 30.4 us -> 13.4 us  [interps(): pl.pallas_call(functools.partial(interp_kernel, levels), out_shape=(jax.S...]
    pallas_call x1, Pallas kernels: 18.1 us -> 10.3 us  [factor_inverse(): pl.pallas_call(factor_kernel, out_shape=jax.ShapeDtypeStruct((total, tota...]
    another operation x0 -> x6, local copies, waits for them, and re-layouts: none -> 4.34 us  [the longest x5 2.95 us: pick2(): index[:, None]]
    ppermute x12, waiting for transfers between devices: 20.6 us -> 19.2 us  [from_partner(): lax.ppermute(block, axis, [(i, i ^ 1 << apart) for i in range(count)])]
    unnamed x42 -> x44, local copies, waits for them, and re-layouts: 4.94 us -> 4.94 us
  transfers between devices with their start and end apart: 15 -> 15, of which waited for: 7 -> 7; matrix products, arithmetic and copies ran while one was open for 12% -> 18% of each run, Pallas kernels for 15% -> 10%
where the time goes in v2:
time: 99.9 us; the launch traced here: 99.5 us
  Pallas kernels  34.6 us (35%)
  waiting for transfers between devices  27.9 us (28%)
  matrix products  12.4 us (12%)
  local copies, waits for them, and re-layouts  9.39 us (9%)
  starting transfers between devices  8.91 us (9%)
  other arithmetic  5.29 us (5%)
    ppermute x12, waiting for transfers between devices, from_partner(): lax.ppermute(block, axis, [(i, i ^ 1 << apart) for i in range(count)])  19.2 us
    pallas_call x1, Pallas kernels, interps(): pl.pallas_call(functools.partial(interp_kernel, levels), out_shape=(jax.S...  13.4 us
    pallas_call x1, Pallas kernels, factor_inverse(): pl.pallas_call(factor_kernel, out_shape=jax.ShapeDtypeStruct((total, tota...  10.3 us
    ppermute x3, waiting for transfers between devices, shifted(): lax.ppermute(block, axis, [((i - distance) % count, i) for i in range(cou...  8.67 us
    pallas_call x4, Pallas kernels, pick2(): pl.pallas_call(pick2_kernel, out_shape=jax.ShapeDtypeStruct(own.shape, f3...  8.26 us
    ppermute x3, starting transfers between devices, shifted(): lax.ppermute(block, axis, [((i - distance) % count, i) for i in range(cou...  6.78 us
    unnamed x44, local copies, waits for them, and re-layouts  4.94 us
    dot_general x4, matrix products, per_device(): lax.dot_general(jnp.concatenate([current, sibling], axis=0), picked, cont...  4.56 us
  transfers between devices with their start and end apart: 15, of which 7 were waited for; matrix products, arithmetic and copies ran while one was open for 18% of the time, Pallas kernels for 10%

profile of v2, /device:TPU:0, one launch (start us, length us, event | category | flops | bytes accessed | tf_op | source)
XLA Modules:
  0.0 99.5 jit_solution(15021080865319568524)
XLA Ops:
  1.2 6.5 %collective-permute-start.1 = (bf16[512,512]{1,0:T(8,128)(2,1)}, bf16[512,512]{1,0:T(8,128)(2,1)S(1)}, u32[]{:S(2)}, u32[]{:S(2)}) collective-permute-start(bf16[512,512]{1,0:T(8,128)(2,1)} %param.9), channel_id=1, source_target_pairs={{2,0},{4,2},{6,4},{8,6},{10,8},{12,10},{14,12},{16,14},{18,16},{20... | collective-permute-start | bytes 1572872 | tf_op jit(solution)/shard_map/ppermute | solution.py:20
  8.3 1.4 %copy.16.index_ref = s32[128,1]{1,0:T(8,128)} copy(s32[128,1]{0,1:T(1,128)} %bitcast.59) | data formatting | bytes 1024 | tf_op jit(solution)/shard_map/broadcast_in_dim;squeeze | solution.py:124
  9.7 1.9 %maximum_bitcast_fusion = bf16[1,512,512]{2,1,0:T(8,128)(2,1)} fusion(bf16[256,512]{1,0:T(8,128)(2,1)} %param.13, bf16[256,512]{1,0:T(8,128)(2,1)} %param.12), kind=kLoop, calls=%fused_computation.13 | loop fusion | flops 1048576 | bytes 1048576 | tf_op jit(solution)/shard_map/broadcast_in_dim | solution.py:216
  13.1 10.3 %factor_inverse.1 = f32[256,256]{1,0:T(8,128)} custom-call(f32[256,128]{1,0:T(8,128)} %pad_maximum_fusion.7.diag_ref, f32[256,128]{1,0:T(8,128)} %pad_maximum_fusion.8.sub_ref), custom_call_target="tpu_custom_call" | custom-call | flops 4000000000 | bytes 1000000 | tf_op jit(solution)/shard_map/factor_inverse/pallas_call | solution.py:95
  28.7 8.7 %collective-permute-done.6 = bf16[128,512]{1,0:T(8,128)(2,1)S(1)} collective-permute-done((bf16[128,512]{1,0:T(8,128)(2,1)S(1)}, bf16[128,512]{1,0:T(8,128)(2,1)S(1)}, u32[]{:S(2)}, u32[]{:S(2)}) %collective-permute-start.6) | collective-permute-done | bytes 131104 | tf_op jit(solution)/shard_map/ppermute | solution.py:20
  37.8 1.0 collective-permute-done.7
  39.2 1.7 %fusion.1 = f32[512,512]{0,1:T(8,128)} fusion(f32[512,512]{0,1:T(8,128)S(1)} %fusion.10, f32[512,512]{0,1:T(8,128)S(1)} %fusion.37, f32[512,512]{0,1:T(8,128)S(1)} %fusion.3, bf16[512,1024]{1,0:T(8,128)(2,1)S(1)} %copy-done.9, bf16[512,512]{1,0:T(8,128)(2,1)S(1)} %get-tuple-element.8, bf16[512,512]{1,0:T(8,128)(2,1)S(1)} %get-tuple-element.7), kind=kOutput, calls=%fused_computation.2 | convolution fusion | flops 539754496 | bytes 6291456 | tf_op jit(solution)/shard_map/dot_general | solution.py:194
  40.8 2.7 %pick_rows.1 = f32[128,512]{1,0:T(8,128)} custom-call(s32[128,1]{1,0:T(8,128)} %copy.16.index_ref, s32[1]{0:T(128)} %bitcast.8.low_ref, f32[512,512]{1,0:T(8,128)} %bitcast.57), custom_call_target="tpu_custom_call" | custom-call | flops 100000000 | bytes 1000000 | tf_op jit(solution)/shard_map/pick_rows/pallas_call | solution.py:117
  43.9 1.3 %collective-permute-done.9 = f32[128,512]{1,0:T(8,128)S(1)} collective-permute-done((f32[128,512]{1,0:T(8,128)}, f32[128,512]{1,0:T(8,128)S(1)}, u32[]{:S(2)}, u32[]{:S(2)}) %collective-permute-start.9) | collective-permute-done | bytes 262176 | tf_op jit(solution)/shard_map/ppermute | solution.py:25
  45.3 1.0 add.36
  47.1 5.0 %collective-permute-done.10.sib_ref = f32[128,256]{1,0:T(8,128)S(1)} collective-permute-done((f32[128,256]{1,0:T(8,128)S(1)}, f32[128,256]{1,0:T(8,128)S(1)}, u32[]{:S(2)}, u32[]{:S(2)}) %collective-permute-start.10) | collective-permute-done | bytes 131104 | tf_op jit(solution)/shard_map/ppermute | solution.py:25
  52.8 2.1 %pick_merged.4.own_ref = f32[128,256]{1,0:T(8,128)} custom-call(s32[128,1]{1,0:T(8,128)} %copy.17.index_ref, f32[128,256]{1,0:T(8,128)} %copy-done.6, f32[128,256]{1,0:T(8,128)} %copy-done.12), custom_call_target="tpu_custom_call" | custom-call | flops 100000000 | bytes 1000000 | tf_op jit(solution)/shard_map/pick_merged/pallas_call | solution.py:136
  55.6 4.4 %collective-permute-done.11.sib_ref = f32[128,256]{1,0:T(8,128)S(1)} collective-permute-done((f32[128,256]{1,0:T(8,128)}, f32[128,256]{1,0:T(8,128)S(1)}, u32[]{:S(2)}, u32[]{:S(2)}) %collective-permute-start.11) | collective-permute-done | bytes 131104 | tf_op jit(solution)/shard_map/ppermute | solution.py:25
  60.7 2.1 %pick_merged.5.own_ref = f32[128,256]{1,0:T(8,128)} custom-call(s32[128,1]{1,0:T(8,128)} %copy.18.index_ref, f32[128,256]{1,0:T(8,128)} %pick_merged.4.own_ref, f32[128,256]{1,0:T(8,128)} %copy-done.13), custom_call_target="tpu_custom_call" | custom-call | flops 100000000 | bytes 1000000 | tf_op jit(solution)/shard_map/pick_merged/pallas_call | solution.py:136
  64.3 1.4 %convolution_bitcast_fusion.3 = f32[1,256,128]{2,1,0:T(8,128)S(1)} fusion(f32[128,256]{1,0:T(8,128)} %pick_merged.4.own_ref, f32[128,256]{1,0:T(8,128)} %copy-done.12, f32[128,256]{1,0:T(8,128)} %copy-done.6), kind=kOutput, calls=%fused_computation.8 | convolution fusion | flops 100728832 | bytes 524288 | tf_op jit(solution)/shard_map/dot_general | solution.py:254
  65.7 2.3 %collective-permute-done.12.sib_ref = f32[128,256]{1,0:T(8,128)S(1)} collective-permute-done((f32[128,256]{1,0:T(8,128)}, f32[128,256]{1,0:T(8,128)S(1)}, u32[]{:S(2)}, u32[]{:S(2)}) %collective-permute-start.12) | collective-permute-done | bytes 131104 | tf_op jit(solution)/shard_map/ppermute | solution.py:25
  68.6 2.1 %pick_merged.6.own_ref = f32[128,256]{1,0:T(8,128)} custom-call(s32[128,1]{1,0:T(8,128)} %copy.19.index_ref, f32[128,256]{1,0:T(8,128)} %pick_merged.5.own_ref, f32[128,256]{1,0:T(8,128)} %copy-done.15), custom_call_target="tpu_custom_call" | custom-call | flops 100000000 | bytes 1000000 | tf_op jit(solution)/shard_map/pick_merged/pallas_call | solution.py:136
  71.1 1.3 %convolution_bitcast_fusion.1 = f32[1,256,128]{2,1,0:T(8,128)S(1)} fusion(f32[128,256]{1,0:T(8,128)} %pick_merged.6.own_ref, f32[128,256]{1,0:T(8,128)} %copy-done.15, f32[128,256]{1,0:T(8,128)S(1)} %copy-done.4), kind=kOutput, calls=%fused_computation.6 | convolution fusion | flops 100728832 | bytes 524288 | tf_op jit(solution)/shard_map/dot_general | solution.py:254
  72.5 5.2 %collective-permute-done.13.sib_ref = f32[128,256]{1,0:T(8,128)S(1)} collective-permute-done((f32[128,256]{1,0:T(8,128)}, f32[128,256]{1,0:T(8,128)S(1)}, u32[]{:S(2)}, u32[]{:S(2)}) %collective-permute-start.13) | collective-permute-done | bytes 131104 | tf_op jit(solution)/shard_map/ppermute | solution.py:25
  78.3 2.1 %pick_merged.7 = f32[128,256]{1,0:T(8,128)} custom-call(s32[128,1]{1,0:T(8,128)} %copy.20.index_ref, f32[128,256]{1,0:T(8,128)} %pick_merged.6.own_ref, f32[128,256]{1,0:T(8,128)} %copy-done.16), custom_call_target="tpu_custom_call" | custom-call | flops 100000000 | bytes 1000000 | tf_op jit(solution)/shard_map/pick_merged/pallas_call | solution.py:136
  80.3 1.4 %convolution_bitcast_fusion = f32[1,256,128]{2,1,0:T(8,128)S(1)} fusion(f32[128,256]{1,0:T(8,128)} %pick_merged.7, f32[128,256]{1,0:T(8,128)} %copy-done.16, f32[128,256]{1,0:T(8,128)S(1)} %copy-done.5), kind=kOutput, calls=%fused_computation.5 | convolution fusion | flops 100728832 | bytes 524288 | tf_op jit(solution)/shard_map/dot_general | solution.py:254
  82.5 1.0 fusion.38.gram_ref
  83.5 1.7 %fusion.39.cross_ref = f32[512,128]{1,0:T(8,128)} fusion(f32[512,512]{0,1:T(8,128)S(1)} %copy-done.1, f32[128,512]{1,0:T(8,128)S(1)} %add.36), kind=kOutput, calls=%fused_computation.80 | convolution fusion | flops 402653184 | bytes 1572864 | tf_op jit(solution)/shard_map/dot_general | solution.py:241
  86.1 13.4 %interps.1 = (f32[512,128]{1,0:T(8,128)}, f32[4,256,128]{2,1,0:T(8,128)}) custom-call(s32[4,128]{1,0:T(4,128)} %copy-done.19, s32[4]{0:T(128)} %shift-right-arithmetic_and_fusion.upper_ref, f32[128,128]{1,0:T(8,128)} %fusion.38.gram_ref, f32[512,128]{1,0:T(8,128)} %fusion.39.cross_ref, f32[4,256,128]{2,1,0:T(8,128)} %copy-done.11, f32[4,256,128]{2,1,0:T(8,128)} %copy-done.21), custom_call_target="tpu_custom_call" | custom-call | flops 4000000000 | bytes 1000000 | tf_op jit(solution)/shard_map/interps/pallas_call | solution.py:178
  (93 shorter events, 16.7 us)
Async XLA Ops:
  0.6 27.4 %copy-start = (bf16[512,1024]{1,0:T(8,128)(2,1)S(1)}, bf16[512,1024]{1,0:T(8,128)(2,1)}, u32[]{:S(2)}) copy-start(bf16[512,1024]{1,0:T(8,128)(2,1)} %param.10) | copy-start | bytes 3145732
  0.6 11.0 %copy-start.18 = (f32[128,128]{1,0:T(8,128)S(1)}, f32[128,128]{1,0:T(8,128)}, u32[]{:S(2)}) copy-start(f32[128,128]{1,0:T(8,128)} %param.14) | copy-start | bytes 196612
  0.7 11.0 %copy-start.17 = (f32[128,128]{1,0:T(8,128)S(1)}, f32[128,128]{1,0:T(8,128)}, u32[]{:S(2)}) copy-start(f32[128,128]{1,0:T(8,128)} %param.15) | copy-start | bytes 196612
  0.7 23.3 %collective-permute-start = (bf16[512,512]{1,0:T(8,128)(2,1)}, bf16[512,512]{1,0:T(8,128)(2,1)S(1)}, u32[]{:S(2)}, u32[]{:S(2)}) collective-permute-start(bf16[512,512]{1,0:T(8,128)(2,1)} %param.9), channel_id=1, source_target_pairs={{0,1},{1,0},{2,3},{3,2},{4,5},{5,4},{6,7},{7,6},{8,9},{9,8},{10,11... | collective-permute-start | bytes 1572872 | tf_op jit(solution)/shard_map/ppermute | solution.py:25
  1.2 22.1 %collective-permute-start.1 = (bf16[512,512]{1,0:T(8,128)(2,1)}, bf16[512,512]{1,0:T(8,128)(2,1)S(1)}, u32[]{:S(2)}, u32[]{:S(2)}) collective-permute-start(bf16[512,512]{1,0:T(8,128)(2,1)} %param.9), channel_id=1, source_target_pairs={{2,0},{4,2},{6,4},{8,6},{10,8},{12,10},{14,12},{16,14},{18,16},{20... | collective-permute-start | bytes 1572872 | tf_op jit(solution)/shard_map/ppermute | solution.py:20
  7.8 3.8 %collective-permute-start.3 = (f32[128,128]{1,0:T(8,128)}, f32[128,128]{1,0:T(8,128)S(1)}, u32[]{:S(2)}, u32[]{:S(2)}) collective-permute-start(f32[128,128]{1,0:T(8,128)} %param.14), channel_id=1, source_target_pairs={{0,1},{1,0},{2,3},{3,2},{4,5},{5,4},{6,7},{7,6},{8,9},{9,8},{10,11... | collective-permute-start | bytes 196616 | tf_op jit(solution)/shard_map/ppermute | solution.py:25
  7.9 3.8 %collective-permute-start.4 = (f32[128,128]{1,0:T(8,128)}, f32[128,128]{1,0:T(8,128)S(1)}, u32[]{:S(2)}, u32[]{:S(2)}) collective-permute-start(f32[128,128]{1,0:T(8,128)} %param.15), channel_id=1, source_target_pairs={{0,1},{1,0},{2,3},{3,2},{4,5},{5,4},{6,7},{7,6},{8,9},{9,8},{10,11... | collective-permute-start | bytes 196616 | tf_op jit(solution)/shard_map/ppermute | solution.py:25
  8.3 30.5 %collective-permute-start.8 = (bf16[256,512]{1,0:T(8,128)(2,1)}, bf16[256,512]{1,0:T(8,128)(2,1)S(1)}, u32[]{:S(2)}, u32[]{:S(2)}) collective-permute-start(bf16[256,512]{1,0:T(8,128)(2,1)} %param.13), channel_id=1, source_target_pairs={{30,0},{0,2},{2,4},{4,6},{6,8},{8,10},{10,12},{12,14},{14,16},{16,... | collective-permute-start | bytes 786440 | tf_op jit(solution)/shard_map/ppermute | solution.py:20
  11.5 12.1 %collective-permute-start.5 = (bf16[1,512,512]{2,1,0:T(8,128)(2,1)}, bf16[1,512,512]{2,1,0:T(8,128)(2,1)S(1)}, u32[]{:S(2)}, u32[]{:S(2)}) collective-permute-start(bf16[1,512,512]{2,1,0:T(8,128)(2,1)} %maximum_bitcast_fusion), channel_id=1, source_target_pairs={{0,1},{1,0},{2,3},{3,2},{4,5},{5,4},{6,7},{7,6},{8,9},{9,8},{10,11... | collective-permute-start | bytes 1572872 | tf_op jit(solution)/shard_map/ppermute | solution.py:25
  13.1 10.6 %copy-start.2 = (bf16[256,512]{1,0:T(8,128)(2,1)S(1)}, bf16[256,512]{1,0:T(8,128)(2,1)}, u32[]{:S(2)}) copy-start(bf16[256,512]{1,0:T(8,128)(2,1)} %param.12) | copy-start | bytes 786436
  13.1 10.6 %copy-start.7 = (bf16[256,512]{1,0:T(8,128)(2,1)S(1)}, bf16[256,512]{1,0:T(8,128)(2,1)}, u32[]{:S(2)}) copy-start(bf16[256,512]{1,0:T(8,128)(2,1)} %param.13) | copy-start | bytes 786436
  23.3 2.1 %collective-permute-start.2 = (bf16[512,512]{1,0:T(8,128)(2,1)S(1)}, bf16[512,512]{1,0:T(8,128)(2,1)S(1)}, u32[]{:S(2)}, u32[]{:S(2)}) collective-permute-start(bf16[512,512]{1,0:T(8,128)(2,1)S(1)} %collective-permute-done.1), channel_id=1, source_target_pairs={{0,1},{1,0},{2,3},{3,2},{4,5},{5,4},{6,7},{7,6},{8,9},{9,8},{10,11... | collective-permute-start | bytes 1572872 | tf_op jit(solution)/shard_map/ppermute | solution.py:25
  27.8 9.6 %collective-permute-start.6 = (bf16[128,512]{1,0:T(8,128)(2,1)S(1)}, bf16[128,512]{1,0:T(8,128)(2,1)S(1)}, u32[]{:S(2)}, u32[]{:S(2)}) collective-permute-start(bf16[128,512]{1,0:T(8,128)(2,1)S(1)} %constant_dynamic-slice_fusion.1), channel_id=1, source_target_pairs={{30,0},{0,2},{2,4},{4,6},{6,8},{8,10},{10,12},{12,14},{14,16},{16,... | collective-permute-start | bytes 393224 | tf_op jit(solution)/shard_map/ppermute | solution.py:20
  37.4 1.3 %collective-permute-start.7 = (bf16[128,512]{1,0:T(8,128)(2,1)S(1)}, bf16[128,512]{1,0:T(8,128)(2,1)S(1)}, u32[]{:S(2)}, u32[]{:S(2)}) collective-permute-start(bf16[128,512]{1,0:T(8,128)(2,1)S(1)} %collective-permute-done.6), channel_id=1, source_target_pairs={{0,1},{1,0},{2,3},{3,2},{4,5},{5,4},{6,7},{7,6},{8,9},{9,8},{10,11... | collective-permute-start | bytes 393224 | tf_op jit(solution)/shard_map/ppermute | solution.py:25
  43.5 1.7 %collective-permute-start.9 = (f32[128,512]{1,0:T(8,128)}, f32[128,512]{1,0:T(8,128)S(1)}, u32[]{:S(2)}, u32[]{:S(2)}) collective-permute-start(f32[128,512]{1,0:T(8,128)} %pick_rows.1), channel_id=1, source_target_pairs={{0,1},{1,0},{2,3},{3,2},{4,5},{5,4},{6,7},{7,6},{8,9},{9,8},{10,11... | collective-permute-start | bytes 786440 | tf_op jit(solution)/shard_map/ppermute | solution.py:25
  43.9 18.8 %copy-start.19 = (s32[4,128]{1,0:T(4,128)}, s32[4,128]{1,0:T(4,128)S(1)}, u32[]{:S(2)}) copy-start(s32[4,128]{1,0:T(4,128)S(1)} %add_select_fusion.index_ref) | copy-start | bytes 6148
  46.3 5.8 %collective-permute-start.10 = (f32[128,256]{1,0:T(8,128)S(1)}, f32[128,256]{1,0:T(8,128)S(1)}, u32[]{:S(2)}, u32[]{:S(2)}) collective-permute-start(f32[128,256]{1,0:T(8,128)S(1)} %constant_dynamic-slice_fusion.own_ref), channel_id=1, source_target_pairs={{0,2},{2,0},{4,6},{6,4},{8,10},{10,8},{12,14},{14,12},{16,18},{18,... | collective-permute-start | bytes 393224 | tf_op jit(solution)/shard_map/ppermute | solution.py:25
  54.8 15.9 %copy-start.3 = (f32[128,256]{1,0:T(8,128)S(1)}, f32[128,256]{1,0:T(8,128)}, u32[]{:S(2)}) copy-start(f32[128,256]{1,0:T(8,128)} %pick_merged.4.own_ref) | copy-start | bytes 393220
  54.8 5.2 %collective-permute-start.11 = (f32[128,256]{1,0:T(8,128)}, f32[128,256]{1,0:T(8,128)S(1)}, u32[]{:S(2)}, u32[]{:S(2)}) collective-permute-start(f32[128,256]{1,0:T(8,128)} %pick_merged.4.own_ref), channel_id=1, source_target_pairs={{0,4},{2,6},{4,0},{6,2},{8,12},{10,14},{12,8},{14,10},{16,20},{18,... | collective-permute-start | bytes 393224 | tf_op jit(solution)/shard_map/ppermute | solution.py:25
  62.7 8.0 %copy-start.14 = (f32[128,256]{1,0:T(8,128)S(1)}, f32[128,256]{1,0:T(8,128)}, u32[]{:S(2)}) copy-start(f32[128,256]{1,0:T(8,128)} %copy-done.13) | copy-start | bytes 393220
  62.7 5.2 %collective-permute-start.12 = (f32[128,256]{1,0:T(8,128)}, f32[128,256]{1,0:T(8,128)S(1)}, u32[]{:S(2)}, u32[]{:S(2)}) collective-permute-start(f32[128,256]{1,0:T(8,128)} %pick_merged.5.own_ref), channel_id=1, source_target_pairs={{0,8},{2,10},{4,12},{6,14},{8,0},{10,2},{12,4},{14,6},{16,24},{18,... | collective-permute-start | bytes 393224 | tf_op jit(solution)/shard_map/ppermute | solution.py:25
  70.7 9.7 %copy-start.5 = (f32[128,256]{1,0:T(8,128)S(1)}, f32[128,256]{1,0:T(8,128)}, u32[]{:S(2)}) copy-start(f32[128,256]{1,0:T(8,128)} %pick_merged.6.own_ref) | copy-start | bytes 393220
  70.7 6.9 %collective-permute-start.13 = (f32[128,256]{1,0:T(8,128)}, f32[128,256]{1,0:T(8,128)S(1)}, u32[]{:S(2)}, u32[]{:S(2)}) collective-permute-start(f32[128,256]{1,0:T(8,128)} %pick_merged.6.own_ref), channel_id=1, source_target_pairs={{0,16},{2,18},{4,20},{6,22},{8,24},{10,26},{12,28},{14,30},{16,0},... | collective-permute-start | bytes 393224 | tf_op jit(solution)/shard_map/ppermute | solution.py:25
  81.8 3.4 %collective-permute-start.14 = (f32[4,256,128]{2,1,0:T(8,128)S(1)}, f32[4,256,128]{2,1,0:T(8,128)S(1)}, u32[]{:S(2)}, u32[]{:S(2)}) collective-permute-start(f32[4,256,128]{2,1,0:T(8,128)S(1)} %pad_maximum_fusion.6.mine_ref), channel_id=1, source_target_pairs={{0,1},{1,0},{2,3},{3,2},{4,5},{5,4},{6,7},{7,6},{8,9},{9,8},{10,11... | collective-permute-start | bytes 1572872 | tf_op jit(solution)/shard_map/ppermute | solution.py:25
  (13 other events, 30.2 us)

commit v3 on v2

--- a/solution.py
+++ b/solution.py
@@ -103,62 +103,139 @@
     )(diag, sub)
 
 
-def one_hot(column, first, count):
-    spots = lax.broadcasted_iota(jnp.int32, (column.shape[0], count), 1) + first
-    return jnp.where(column == spots, 1.0, 0.0)
-
-
-def pick_kernel(index_ref, low_ref, source_ref, out_ref):
-    chosen = one_hot(index_ref[...], low_ref[0], source_ref.shape[0])
-    out_ref[...] = jnp.dot(chosen, source_ref[...], precision=highest)
-
-
-def pick(index, low, source):
+MESH = pl.DeviceIdType.MESH
+
+
+def picked_rows(index, parts):
+    first, total = 0, None
+    for part in parts:
+        count, width = part.shape
+        spots = lax.broadcasted_iota(jnp.int32, (count, index.shape[1]), 0) + first
+        marks = jnp.where(spots == index, 1.0, 0.0).T.astype(jnp.bfloat16)
+        high = part.astype(jnp.bfloat16)
+        rest = part - high.astype(f32)
+        middle = rest.astype(jnp.bfloat16)
+        low = (rest - middle.astype(f32)).astype(jnp.bfloat16)
+        value = (
+            jnp.dot(marks, high, preferred_element_type=f32)
+            + jnp.dot(marks, middle, preferred_element_type=f32)
+        ) + jnp.dot(marks, low, preferred_element_type=f32)
+        total = value if total is None else total + value
+        first = first + count
+    return total
+
+
+def tree_kernel(
+    levels, samples_ref, leaf_set_ref, sets_ref, cross_out, gram_out, total_out,
+    contrib, other, chosen, current, sibling, mine, theirs,
+    swap_sem, tree_send, tree_recv, sum_send, sum_recv,
+):
+    leaf, blk = lax.axis_index("leaf"), lax.axis_index("blk")
+    rows = samples_ref.shape[0]
+    width = current.shape[2]
+    mate = (leaf, 1 - blk)
+    above = []
+    for j in range(levels):
+        bit = 1 << j
+        above.append((leaf + bit - 2 * bit * ((leaf // bit) % 2), blk))
+    barrier = pltpu.get_barrier_semaphore()
+    for device in [mate] + above:
+        pl.semaphore_signal(barrier, inc=1, device_id=device, device_id_type=MESH)
+
+    contrib[...] = picked_rows(leaf_set_ref[...] - blk * rows, [samples_ref[...]])
+    pl.semaphore_wait(barrier, levels + 1)
+    swap = pltpu.make_async_remote_copy(
+        src_ref=contrib, dst_ref=other, send_sem=swap_sem.at[0], recv_sem=swap_sem.at[1],
+        device_id=mate, device_id_type=MESH,
+    )
+    swap.start()
+    swap.wait()
+    chosen[...] = contrib[...] + other[...]
+    columns = pl.ds(pl.multiple_of(blk * width, width), width)
+    current[0] = chosen[:, columns]
+    sums = []
+
+    def dots(left, right):
+        return lax.dot_general(
+            left, right, contract_cols, precision=highest, preferred_element_type=f32
+        )
+
+    def partial(j):
+        half = current.shape[1]
+        mine[j, :half, :] = dots(current[j], current[j + 1])
+        mine[j, half:, :] = dots(sibling[j], current[j + 1])
+        copy = pltpu.make_async_remote_copy(
+            src_ref=mine.at[j], dst_ref=theirs.at[j],
+            send_sem=sum_send.at[j], recv_sem=sum_recv.at[j],
+            device_id=mate, device_id_type=MESH,
+        )
+        copy.start()
+        sums.append(copy)
+
+    def finish(j):
+        sums[j].wait()
+        total = mine[j] + theirs[j]
+        total_out[j] = total
+        gram_out[j + 1] = picked_rows(sets_ref[j : j + 1, :], [total])
+
+    for j in range(levels):
+        copy = pltpu.make_async_remote_copy(
+            src_ref=current.at[j], dst_ref=sibling.at[j],
+            send_sem=tree_send.at[j], recv_sem=tree_recv.at[j],
+            device_id=above[j], device_id_type=MESH,
+        )
+        copy.start()
+        if j == 0:
+            gram_out[0] = dots(chosen[...], chosen[...])
+            cross_out[...] = dots(samples_ref[...], chosen[...])
+        else:
+            partial(j - 1)
+        if j > 1:
+            finish(j - 2)
+        copy.wait()
+        current[j + 1] = picked_rows(sets_ref[j : j + 1, :], [current[j], sibling[j]])
+    partial(levels - 1)
+    for j in range(max(levels - 2, 0), levels):
+        finish(j)
+
+
+def tree(samples, leaf_set, sets):
+    levels, rank = sets.shape
+    rows, cols = samples.shape
+    width = cols // lax.axis_size("blk")
     return pl.pallas_call(
-        pick_kernel,
-        out_shape=jax.ShapeDtypeStruct((index.shape[0], source.shape[1]), f32),
-        in_specs=[VMEM_SPEC, SMEM_SPEC, VMEM_SPEC],
-        out_specs=VMEM_SPEC,
-        cost_estimate=pl.CostEstimate(flops=10**8, bytes_accessed=10**6, transcendentals=0),
-        name="pick_rows",
-    )(index[:, None], low.reshape(1), source)
-
-
-def pick2_kernel(index_ref, own_ref, sib_ref, out_ref):
-    half = own_ref.shape[0]
-    index = index_ref[...]
-    out_ref[...] = jnp.dot(
-        one_hot(index, 0, half), own_ref[...], precision=highest
-    ) + jnp.dot(one_hot(index, half, half), sib_ref[...], precision=highest)
-
-
-def pick2(index, own, sib):
-    return pl.pallas_call(
-        pick2_kernel,
-        out_shape=jax.ShapeDtypeStruct(own.shape, f32),
+        functools.partial(tree_kernel, levels),
+        out_shape=(
+            jax.ShapeDtypeStruct((rows, rank), f32),
+            jax.ShapeDtypeStruct((levels + 1, rank, rank), f32),
+            jax.ShapeDtypeStruct((levels, 2 * rank, rank), f32),
+        ),
         in_specs=[VMEM_SPEC] * 3,
-        out_specs=VMEM_SPEC,
-        cost_estimate=pl.CostEstimate(flops=10**8, bytes_accessed=10**6, transcendentals=0),
-        name="pick_merged",
-    )(index[:, None], own, sib)
-
-
-def interp_kernel(
-    levels, index_ref, upper_ref, gram_ref, cross_ref, mine_ref, other_ref,
-    leaf_out, merge_out, total_ref, *work,
-):
-    size = gram_ref.shape[0]
-    work[0][...] = gram_ref[...]
-    for j in range(levels):
-        total_ref[j] = mine_ref[j] + other_ref[j]
-
-        def body(i, _):
-            for u in range(8):
-                at = i * 8 + u
-                work[j + 1][pl.ds(at, 1), :] = total_ref[j, pl.ds(index_ref[j, at], 1), :]
-            return 0
-
-        lax.fori_loop(0, size // 8, body, 0)
+        out_specs=(VMEM_SPEC,) * 3,
+        scratch_shapes=[
+            pltpu.VMEM((rank, cols), f32),
+            pltpu.VMEM((rank, cols), f32),
+            pltpu.VMEM((rank, cols), f32),
+            pltpu.VMEM((levels + 1, rank, width), f32),
+            pltpu.VMEM((levels, rank, width), f32),
+            pltpu.VMEM((levels, 2 * rank, rank), f32),
+            pltpu.VMEM((levels, 2 * rank, rank), f32),
+            pltpu.SemaphoreType.DMA((2,)),
+            pltpu.SemaphoreType.DMA((levels,)),
+            pltpu.SemaphoreType.DMA((levels,)),
+            pltpu.SemaphoreType.DMA((levels,)),
+            pltpu.SemaphoreType.DMA((levels,)),
+        ],
+        compiler_params=pltpu.CompilerParams(collective_id=0, has_side_effects=True),
+        cost_estimate=pl.CostEstimate(flops=10**10, bytes_accessed=10**6, transcendentals=0),
+        name="tree",
+    )(samples, leaf_set, sets)
+
+
+def interp_kernel(levels, upper_ref, gram_ref, cross_ref, total_ref, leaf_out, merge_out, *work):
+    size = gram_ref.shape[1]
+    for j in range(levels + 1):
+        work[j][...] = gram_ref[j]
     invert_in_place(work)
     leaf_out[...] = jnp.dot(
         cross_ref[...], work[0][...], precision=highest, preferred_element_type=f32
@@ -172,22 +249,21 @@
         merge_out[j, pl.ds(pl.multiple_of(size - start, size), size), :] = rows[size:]
 
 
-def interps(index, upper, gram, cross, mine, other):
-    levels = index.shape[0]
-    size = gram.shape[0]
+def interps(upper, gram, cross, total):
+    levels = total.shape[0]
+    size = gram.shape[1]
     return pl.pallas_call(
         functools.partial(interp_kernel, levels),
         out_shape=(
             jax.ShapeDtypeStruct(cross.shape, f32),
-            jax.ShapeDtypeStruct(mine.shape, f32),
+            jax.ShapeDtypeStruct(total.shape, f32),
         ),
-        in_specs=[SMEM_SPEC, SMEM_SPEC] + [VMEM_SPEC] * 4,
+        in_specs=[SMEM_SPEC] + [VMEM_SPEC] * 3,
         out_specs=(VMEM_SPEC, VMEM_SPEC),
-        scratch_shapes=[pltpu.VMEM(mine.shape, f32)]
-        + [pltpu.VMEM((size, size), f32)] * (levels + 1),
+        scratch_shapes=[pltpu.VMEM((size, size), f32)] * (levels + 1),
         cost_estimate=pl.CostEstimate(flops=4 * 10**9, bytes_accessed=10**6, transcendentals=0),
         name="interps",
-    )(index, upper, gram, cross, mine, other)
+    )(upper, gram, cross, total)
 
 
 def bf16_dot(left, right):
@@ -236,32 +312,12 @@
         previous_link, previous_weights, contract_rows, preferred_element_type=f32
     )
     samples = direct - own_back - from_previous
-    contrib = pick(leaf_skeleton[0], blk * rows, samples)
-    chosen = contrib + from_partner(contrib, "blk", 0)
-    leaf_cross = lax.dot_general(samples, chosen, contract_cols, precision=highest)
-    leaf_gram = lax.dot_general(chosen, chosen, contract_cols, precision=highest)
-    width = chosen.shape[1] // blk_count
-    current = lax.dynamic_slice_in_dim(chosen, blk * width, width, 1)
-    rank = chosen.shape[0]
+    rank = leaf_skeleton.shape[1]
     levels = merge_skeleton.shape[1]
     upper = (leaf >> jnp.arange(levels, dtype=jnp.int32)) & 1
     local_sets = (merge_skeleton[0] + rank * upper[:, None]) % (2 * rank)
-    crosses = []
-    for j in range(levels):
-        sibling = from_partner(current, "leaf", j)
-        picked = pick2(local_sets[j], current, sibling)
-        crosses.append(
-            lax.dot_general(
-                jnp.concatenate([current, sibling], axis=0), picked, contract_cols,
-                precision=highest,
-            )
-        )
-        current = picked
-    mine = jnp.stack(crosses, axis=0)
-    other = from_partner(mine, "blk", 0)
-    leaf_interp, merge_interp = interps(
-        local_sets, upper, leaf_gram, leaf_cross, mine, other
-    )
+    leaf_cross, grams, totals = tree(samples, leaf_skeleton, local_sets)
+    leaf_interp, merge_interp = interps(upper, grams, leaf_cross, totals)
     return (samples, leaf_interp, merge_interp[None])
 
 

time: 99.9 us -> 78.9 us (0.79)
  waiting for transfers between devices: 27.9 us -> 9.66 us
  Pallas kernels: 34.6 us -> 48.2 us
  local copies, waits for them, and re-layouts: 9.39 us -> 1.57 us
  matrix products: 12.4 us -> 5.22 us
    ppermute x12 -> x6, waiting for transfers between devices: 19.2 us -> 0.99 us  [from_partner(): lax.ppermute(block, axis, [(i, i ^ 1 << apart) for i in range(count)])]
    pallas_call x5 -> x1, Pallas kernels: 10.9 us -> 25.8 us  [tree(): pl.pallas_call(functools.partial(tree_kernel, levels), out_shape=(jax.Sha...]
    dot_general x6 -> x0, matrix products: 7.26 us -> none  [the longest x4 4.56 us: per_device(): lax.dot_general(jnp.concatenate([current, sibling], axis=0), picked, cont...]
    another operation x6 -> x0, local copies, waits for them, and re-layouts: 4.34 us -> none  [the longest x5 2.95 us: pick2(): index[:, None]]
    unnamed x44 -> x18, local copies, waits for them, and re-layouts: 4.94 us -> 1.48 us
    pallas_call x1, Pallas kernels: 13.4 us -> 12.2 us  [interps(): pl.pallas_call(functools.partial(interp_kernel, levels), out_shape=(jax.S...]
    ppermute x12 -> x6, starting transfers between devices: 2.13 us -> 1.58 us  [from_partner(): lax.ppermute(block, axis, [(i, i ^ 1 << apart) for i in range(count)])]
  transfers between devices with their start and end apart: 15 -> 9, of which waited for: 7 -> 2; matrix products, arithmetic and copies ran while one was open for 18% -> 10% of each run, Pallas kernels for 10% -> 13%
where the time goes in v3:
time: 78.9 us; the launch traced here: 78.6 us
  Pallas kernels  48.2 us (61%)
  waiting for transfers between devices  9.66 us (12%)
  starting transfers between devices  8.36 us (11%)
  matrix products  5.22 us (7%)
  other arithmetic  4.72 us (6%)
  local copies, waits for them, and re-layouts  1.57 us (2%)
  between operations  0.85 us (1%)
    pallas_call x1, Pallas kernels, tree(): pl.pallas_call(functools.partial(tree_kernel, levels), out_shape=(jax.Sha...  25.8 us
    pallas_call x1, Pallas kernels, interps(): pl.pallas_call(functools.partial(interp_kernel, levels), out_shape=(jax.S...  12.2 us
    pallas_call x1, Pallas kernels, factor_inverse(): pl.pallas_call(factor_kernel, out_shape=jax.ShapeDtypeStruct((total, tota...  10.3 us
    ppermute x3, waiting for transfers between devices, shifted(): lax.ppermute(block, axis, [((i - distance) % count, i) for i in range(cou...  8.67 us
    ppermute x3, starting transfers between devices, shifted(): lax.ppermute(block, axis, [((i - distance) % count, i) for i in range(cou...  6.78 us
    dot_general x4, matrix products, bf16_dot(): return jnp.dot(left, right, preferred_element_type=f32)  3.27 us
    broadcast_in_dim x1, other arithmetic, per_device(): links = gathered(jnp.concatenate([link_own, link_next], axis=0)[None])  1.86 us
    ppermute x6, starting transfers between devices, from_partner(): lax.ppermute(block, axis, [(i, i ^ 1 << apart) for i in range(count)])  1.58 us
  transfers between devices with their start and end apart: 9, of which 2 were waited for; matrix products, arithmetic and copies ran while one was open for 10% of the time, Pallas kernels for 13%

profile of v3, /device:TPU:0, one launch (start us, length us, event | category | flops | bytes accessed | tf_op | source)
XLA Modules:
  0.0 78.6 jit_solution(13724831672551776020)
XLA Ops:
  0.7 0.6 collective-permute-start
  1.2 6.5 %collective-permute-start.1 = (bf16[512,512]{1,0:T(8,128)(2,1)}, bf16[512,512]{1,0:T(8,128)(2,1)S(1)}, u32[]{:S(2)}, u32[]{:S(2)}) collective-permute-start(bf16[512,512]{1,0:T(8,128)(2,1)} %param.9), channel_id=1, source_target_pairs={{2,0},{4,2},{6,4},{8,6},{10,8},{12,10},{14,12},{16,14},{18,16},{20... | collective-permute-start | bytes 1572872 | tf_op jit(solution)/shard_map/ppermute | solution.py:20
  7.9 0.3 collective-permute-start.4
  8.3 1.9 %maximum_bitcast_fusion = bf16[1,512,512]{2,1,0:T(8,128)(2,1)} fusion(bf16[256,512]{1,0:T(8,128)(2,1)} %param.13, bf16[256,512]{1,0:T(8,128)(2,1)} %param.12), kind=kLoop, calls=%fused_computation.10 | loop fusion | flops 1048576 | bytes 1048576 | tf_op jit(solution)/shard_map/broadcast_in_dim | solution.py:292
  10.2 0.7 add_select_fusion.sets_ref
  10.8 0.5 shift-right-arithmetic_and_fusion.upper_ref
  11.5 0.7 pad_maximum_fusion.7.sub_ref
  12.2 0.7 pad_maximum_fusion.6.diag_ref
  12.8 10.3 %factor_inverse.1 = f32[256,256]{1,0:T(8,128)} custom-call(f32[256,128]{1,0:T(8,128)} %pad_maximum_fusion.6.diag_ref, f32[256,128]{1,0:T(8,128)} %pad_maximum_fusion.7.sub_ref), custom_call_target="tpu_custom_call" | custom-call | flops 4000000000 | bytes 1000000 | tf_op jit(solution)/shard_map/factor_inverse/pallas_call | solution.py:95
  23.1 0.3 collective-permute-start.2
  23.8 0.9 %copy-done.5 = bf16[512,512]{1,0:T(8,128)(2,1)S(1)} copy-done((bf16[512,512]{1,0:T(8,128)(2,1)S(1)}, bf16[512,512]{1,0:T(8,128)(2,1)}, u32[]{:S(2)}) %copy-start.5) | copy-done | bytes 524312
  24.8 0.4 fusion.3
  25.3 0.4 convolution_add_fusion.1
  25.8 0.5 copy-done.3
  26.3 0.6 fusion.21
  26.9 0.6 convolution_convert_fusion
  27.8 0.7 fusion.4
  28.5 8.7 %collective-permute-done.6 = bf16[128,512]{1,0:T(8,128)(2,1)S(1)} collective-permute-done((bf16[128,512]{1,0:T(8,128)(2,1)S(1)}, bf16[128,512]{1,0:T(8,128)(2,1)S(1)}, u32[]{:S(2)}, u32[]{:S(2)}) %collective-permute-start.6) | collective-permute-done | bytes 131104 | tf_op jit(solution)/shard_map/ppermute | solution.py:20
  37.2 0.4 fusion.22
  37.6 1.0 %collective-permute-done.7 = bf16[128,512]{1,0:T(8,128)(2,1)S(1)} collective-permute-done((bf16[128,512]{1,0:T(8,128)(2,1)S(1)}, bf16[128,512]{1,0:T(8,128)(2,1)S(1)}, u32[]{:S(2)}, u32[]{:S(2)}) %collective-permute-start.7) | collective-permute-done | bytes 131104 | tf_op jit(solution)/shard_map/ppermute | solution.py:25
  38.6 0.3 fusion.11
  38.9 1.7 %fusion.2.samples_ref = f32[512,512]{1,0:T(8,128)} fusion(f32[512,512]{0,1:T(8,128)S(1)} %fusion.11, f32[512,512]{0,1:T(8,128)S(1)} %fusion.22, f32[512,512]{0,1:T(8,128)S(1)} %fusion.4, bf16[512,1024]{1,0:T(8,128)(2,1)S(1)} %copy-done.4, bf16[512,512]{1,0:T(8,128)(2,1)S(1)} %get-tuple-element.14, bf16[512,512]{1,0:T(8,128)(2,1)S(1)} %get-tuple-element.13), kind=kOutput, calls=%fused_computation.3 | convolution fusion | flops 539754496 | bytes 6291456 | tf_op jit(solution)/shard_map/dot_general | solution.py:270
  40.6 25.8 %tree.1 = (f32[512,128]{1,0:T(8,128)}, f32[5,128,128]{2,1,0:T(8,128)}, f32[4,256,128]{2,1,0:T(8,128)}) custom-call(f32[512,512]{1,0:T(8,128)} %fusion.2.samples_ref, s32[1,128]{1,0:T(1,128)} %leaf_set_ref.1, s32[4,128]{1,0:T(4,128)} %add_select_fusion.sets_ref), custom_call_target="tpu_custom_call" | custom-call | flops 10000000000 | bytes 1000000 | tf_op jit(solution)/shard_map/tree/pallas_call | solution.py:206
  66.5 12.2 %interps.1 = (f32[512,128]{1,0:T(8,128)}, f32[4,256,128]{2,1,0:T(8,128)}) custom-call(s32[4]{0:T(128)} %shift-right-arithmetic_and_fusion.upper_ref, f32[5,128,128]{2,1,0:T(8,128)} %get-tuple-element.8.gram_ref, f32[512,128]{1,0:T(8,128)} %get-tuple-element.9.cross_ref, f32[4,256,128]{2,1,0:T(8,128)} %get-tuple-element.10.total_ref), custom_call_target="tpu_custom_call" | custom-call | flops 4000000000 | bytes 1000000 | tf_op jit(solution)/shard_map/interps/pallas_call | solution.py:255
  (36 shorter events, 1.1 us)
Async XLA Ops:
  0.6 27.2 %copy-start = (bf16[512,1024]{1,0:T(8,128)(2,1)S(1)}, bf16[512,1024]{1,0:T(8,128)(2,1)}, u32[]{:S(2)}) copy-start(bf16[512,1024]{1,0:T(8,128)(2,1)} %param.10) | copy-start | bytes 3145732
  0.6 10.8 %copy-start.7 = (f32[128,128]{1,0:T(8,128)S(1)}, f32[128,128]{1,0:T(8,128)}, u32[]{:S(2)}) copy-start(f32[128,128]{1,0:T(8,128)} %param.14) | copy-start | bytes 196612
  0.7 10.8 %copy-start.6 = (f32[128,128]{1,0:T(8,128)S(1)}, f32[128,128]{1,0:T(8,128)}, u32[]{:S(2)}) copy-start(f32[128,128]{1,0:T(8,128)} %param.15) | copy-start | bytes 196612
  0.7 9.5 %copy-start.8 = (s32[1,4,128]{2,1,0:T(4,128)S(1)}, s32[1,4,128]{2,1,0:T(4,128)}, u32[]{:S(2)}) copy-start(s32[1,4,128]{2,1,0:T(4,128)} %param.17) | copy-start | bytes 6148
  0.7 23.1 %collective-permute-start = (bf16[512,512]{1,0:T(8,128)(2,1)}, bf16[512,512]{1,0:T(8,128)(2,1)S(1)}, u32[]{:S(2)}, u32[]{:S(2)}) collective-permute-start(bf16[512,512]{1,0:T(8,128)(2,1)} %param.9), channel_id=1, source_target_pairs={{0,1},{1,0},{2,3},{3,2},{4,5},{5,4},{6,7},{7,6},{8,9},{9,8},{10,11... | collective-permute-start | bytes 1572872 | tf_op jit(solution)/shard_map/ppermute | solution.py:25
  1.2 21.9 %collective-permute-start.1 = (bf16[512,512]{1,0:T(8,128)(2,1)}, bf16[512,512]{1,0:T(8,128)(2,1)S(1)}, u32[]{:S(2)}, u32[]{:S(2)}) collective-permute-start(bf16[512,512]{1,0:T(8,128)(2,1)} %param.9), channel_id=1, source_target_pairs={{2,0},{4,2},{6,4},{8,6},{10,8},{12,10},{14,12},{16,14},{18,16},{20... | collective-permute-start | bytes 1572872 | tf_op jit(solution)/shard_map/ppermute | solution.py:20
  7.8 3.5 %collective-permute-start.3 = (f32[128,128]{1,0:T(8,128)}, f32[128,128]{1,0:T(8,128)S(1)}, u32[]{:S(2)}, u32[]{:S(2)}) collective-permute-start(f32[128,128]{1,0:T(8,128)} %param.14), channel_id=1, source_target_pairs={{0,1},{1,0},{2,3},{3,2},{4,5},{5,4},{6,7},{7,6},{8,9},{9,8},{10,11... | collective-permute-start | bytes 196616 | tf_op jit(solution)/shard_map/ppermute | solution.py:25
  7.9 3.5 %collective-permute-start.4 = (f32[128,128]{1,0:T(8,128)}, f32[128,128]{1,0:T(8,128)S(1)}, u32[]{:S(2)}, u32[]{:S(2)}) collective-permute-start(f32[128,128]{1,0:T(8,128)} %param.15), channel_id=1, source_target_pairs={{0,1},{1,0},{2,3},{3,2},{4,5},{5,4},{6,7},{7,6},{8,9},{9,8},{10,11... | collective-permute-start | bytes 196616 | tf_op jit(solution)/shard_map/ppermute | solution.py:25
  8.3 30.3 %collective-permute-start.8 = (bf16[256,512]{1,0:T(8,128)(2,1)}, bf16[256,512]{1,0:T(8,128)(2,1)S(1)}, u32[]{:S(2)}, u32[]{:S(2)}) collective-permute-start(bf16[256,512]{1,0:T(8,128)(2,1)} %param.13), channel_id=1, source_target_pairs={{30,0},{0,2},{2,4},{4,6},{6,8},{8,10},{10,12},{12,14},{14,16},{16,... | collective-permute-start | bytes 786440 | tf_op jit(solution)/shard_map/ppermute | solution.py:20
  11.3 12.1 %collective-permute-start.5 = (bf16[1,512,512]{2,1,0:T(8,128)(2,1)}, bf16[1,512,512]{2,1,0:T(8,128)(2,1)S(1)}, u32[]{:S(2)}, u32[]{:S(2)}) collective-permute-start(bf16[1,512,512]{2,1,0:T(8,128)(2,1)} %maximum_bitcast_fusion), channel_id=1, source_target_pairs={{0,1},{1,0},{2,3},{3,2},{4,5},{5,4},{6,7},{7,6},{8,9},{9,8},{10,11... | collective-permute-start | bytes 1572872 | tf_op jit(solution)/shard_map/ppermute | solution.py:25
  12.8 10.6 %copy-start.1 = (bf16[256,512]{1,0:T(8,128)(2,1)S(1)}, bf16[256,512]{1,0:T(8,128)(2,1)}, u32[]{:S(2)}) copy-start(bf16[256,512]{1,0:T(8,128)(2,1)} %param.12) | copy-start | bytes 786436
  12.8 10.6 %copy-start.2 = (bf16[256,512]{1,0:T(8,128)(2,1)S(1)}, bf16[256,512]{1,0:T(8,128)(2,1)}, u32[]{:S(2)}) copy-start(bf16[256,512]{1,0:T(8,128)(2,1)} %param.13) | copy-start | bytes 786436
  23.1 2.1 %collective-permute-start.2 = (bf16[512,512]{1,0:T(8,128)(2,1)S(1)}, bf16[512,512]{1,0:T(8,128)(2,1)S(1)}, u32[]{:S(2)}, u32[]{:S(2)}) collective-permute-start(bf16[512,512]{1,0:T(8,128)(2,1)S(1)} %collective-permute-done.1), channel_id=1, source_target_pairs={{0,1},{1,0},{2,3},{3,2},{4,5},{5,4},{6,7},{7,6},{8,9},{9,8},{10,11... | collective-permute-start | bytes 1572872 | tf_op jit(solution)/shard_map/ppermute | solution.py:25
  23.7 1.0 %copy-start.5 = (bf16[512,512]{1,0:T(8,128)(2,1)S(1)}, bf16[512,512]{1,0:T(8,128)(2,1)}, u32[]{:S(2)}) copy-start(bf16[512,512]{1,0:T(8,128)(2,1)} %param.9) | copy-start | bytes 1572868
  25.3 1.0 %copy-start.3 = (f32[256,256]{1,0:T(8,128)S(1)}, f32[256,256]{1,0:T(8,128)}, u32[]{:S(2)}) copy-start(f32[256,256]{1,0:T(8,128)} %factor_inverse.1) | copy-start | bytes 786436
  27.6 9.6 %collective-permute-start.6 = (bf16[128,512]{1,0:T(8,128)(2,1)S(1)}, bf16[128,512]{1,0:T(8,128)(2,1)S(1)}, u32[]{:S(2)}, u32[]{:S(2)}) collective-permute-start(bf16[128,512]{1,0:T(8,128)(2,1)S(1)} %constant_dynamic-slice_fusion), channel_id=1, source_target_pairs={{30,0},{0,2},{2,4},{4,6},{6,8},{8,10},{10,12},{12,14},{14,16},{16,... | collective-permute-start | bytes 393224 | tf_op jit(solution)/shard_map/ppermute | solution.py:20
  37.2 1.3 %collective-permute-start.7 = (bf16[128,512]{1,0:T(8,128)(2,1)S(1)}, bf16[128,512]{1,0:T(8,128)(2,1)S(1)}, u32[]{:S(2)}, u32[]{:S(2)}) collective-permute-start(bf16[128,512]{1,0:T(8,128)(2,1)S(1)} %collective-permute-done.6), channel_id=1, source_target_pairs={{0,1},{1,0},{2,3},{3,2},{4,5},{5,4},{6,7},{7,6},{8,9},{9,8},{10,11... | collective-permute-start | bytes 393224 | tf_op jit(solution)/shard_map/ppermute | solution.py:25
  37.6 1.4 %copy-start.4 = (bf16[512,1024]{1,0:T(8,128)(2,1)S(1)}, bf16[512,1024]{1,0:T(8,128)(2,1)}, u32[]{:S(2)}) copy-start(bf16[512,1024]{1,0:T(8,128)(2,1)} %param.11) | copy-start | bytes 3145732
